TPU v7x, 32 devices: a whole 2x2x4 slice. The times are simulated.
32 devices in a mesh: grp: 8 (over z, x), wide: 4 (over y, core).
Axes of the slice: x: 2, y: 2, z: 4, core: 2. Of those that a mesh axis runs over, the one named last changes fastest.
Arguments:
- velocity: float32 [3, 512, 32, 128], P(None, 'grp', 'wide'), may hold values from -6 to 6
- coarse_ghost: float32 [3, 512, 8, 128], P(None, 'grp', 'wide'), may hold values from -6 to 6
- viscosity: float32 [512, 32, 128], P('grp', 'wide'), may hold values from 0.5 to 4
- stress: float32 [6, 512, 32, 128], P(None, 'grp', 'wide'), may hold values from -6 to 6
- patch_mask: int32 [8, 8], P('grp', 'wide'), may hold values 0 or 1
- coarse_owner: int32 [8, 8], P('grp', 'wide'), may hold values from 0 to 63, as said below
Outputs:
- new_velocity: float32 [3, 512, 32, 128], P(None, 'grp', 'wide')
- coarse_patch_update: float32 [8, 64, 3, 6144], P('grp', 'wide')
Inputs may be any that keep to these rules, and one draw needn't show every extreme that they name: `coarse_owner`: coarse patch c belongs to wide index c // 16. Of the 2 fine patches of one device at most 1 have coarse patches on any one wide index, and in every draw every device sends exactly 1 to one common wide index.
All inputs are finite; a program needn't handle non-finite values. No bound on the sum of `patch_mask` on one device may be relied on, other than what follows from the above.
Results may differ from a plain program's by a relative error of at most 0.000096.
Values sent between devices are 32-bit elements; how exact they have to be, the bound alone decides.
No kernel may reach another device: no remote copies, remote signals or barrier semaphores. Data moves between devices by JAX's collectives and lax.ppermute only.
A program may use at most 128 MiB of HBM per device.

v0:
```python
import jax
import jax.numpy as jnp
from jax import lax
from jax.sharding import PartitionSpec as P

PATCH = 64
CY = 8
P_SIZE = 2
CP_DEV = 16
SWEEPS = 3
PV = 6144


KAPPA = 1.0
OMEGA = 0.8


def with_halo(block, sides, width):
    for axis, dim in sides:
        count = lax.axis_size(axis)
        forward = [(i, i + 1) for i in range(count - 1)]
        backward = [(target, source) for source, target in forward]
        low = lax.ppermute(
            lax.slice_in_dim(block, block.shape[dim] - width, None, axis=dim), axis, forward
        )
        high = lax.ppermute(lax.slice_in_dim(block, 0, width, axis=dim), axis, backward)
        block = jnp.concatenate([low, block, high], axis=dim)
    return block


def y_neighbours(field, low, high):
    ypos = lax.broadcasted_iota(jnp.int32, field.shape, field.ndim - 2)
    last_row = field.shape[-2] - 1
    north = jnp.where(ypos == last_row, jnp.expand_dims(high, -2), jnp.roll(field, -1, axis=-2))
    south = jnp.where(ypos == 0, jnp.expand_dims(low, -2), jnp.roll(field, 1, axis=-2))
    return (north, south)


def apply_operator(values_x, ghost_rows, visc_x):
    centre_cell = visc_x[1:-1]
    visc_east = 0.5 * (centre_cell + visc_x[2:])
    visc_west = 0.5 * (centre_cell + visc_x[:-2])
    visc_n, visc_s = y_neighbours(centre_cell, centre_cell[:, 0, :], centre_cell[:, -1, :])
    visc_north = 0.5 * (centre_cell + visc_n)
    visc_south = 0.5 * (centre_cell + visc_s)
    visc_up = 0.5 * (centre_cell + jnp.roll(centre_cell, -1, axis=2))
    visc_down = 0.5 * (centre_cell + jnp.roll(centre_cell, 1, axis=2))
    interior = values_x[:, 1:-1]
    north_vals, south_vals = y_neighbours(interior, ghost_rows[:, :, 0, :], ghost_rows[:, :, 1, :])
    diffusion = visc_east * (values_x[:, 2:] - interior) - visc_west * (interior - values_x[:, :-2])
    diffusion = (
        diffusion + visc_north * (north_vals - interior) - visc_south * (interior - south_vals)
    )
    diffusion = (
        diffusion
        + visc_up * (jnp.roll(interior, -1, axis=3) - interior)
        - visc_down * (interior - jnp.roll(interior, 1, axis=3))
    )
    diagonal = KAPPA + visc_east + visc_west + visc_north + visc_south + visc_up + visc_down
    return (KAPPA * interior - diffusion, diagonal)


def divergence(stress_x):

    def diff_x(comp):
        return 0.5 * (comp[2:] - comp[:-2])

    def diff_y(comp):
        middle = comp[1:-1]
        zeros_row = jnp.zeros_like(middle[:, 0, :])
        north_vals, south_vals = y_neighbours(middle, zeros_row, zeros_row)
        return 0.5 * (north_vals - south_vals)

    def diff_z(comp):
        middle = comp[1:-1]
        return 0.5 * (jnp.roll(middle, -1, axis=2) - jnp.roll(middle, 1, axis=2))

    force_x = diff_x(stress_x[0]) + diff_y(stress_x[3]) + diff_z(stress_x[4])
    force_y = diff_x(stress_x[3]) + diff_y(stress_x[1]) + diff_z(stress_x[5])
    force_z = diff_x(stress_x[4]) + diff_y(stress_x[5]) + diff_z(stress_x[2])
    return jnp.stack([force_x, force_y, force_z], axis=0)


def patch_data(residual, smoothed, viscosity, coarse_ghost, groups):
    half = PATCH // 2
    blocks = residual.reshape(3, groups, half, 2, CY // 2, 2, P_SIZE, half, 2).mean(axis=(3, 5, 8))
    blocks = jnp.transpose(blocks, (1, 4, 0, 2, 3, 5)).reshape(
        groups, P_SIZE, 3, half * (CY // 2) * half
    )
    flux_low = viscosity[:, 0, :] * (smoothed[:, :, 0, :] - coarse_ghost[:, :, 0, :])
    flux_high = viscosity[:, -1, :] * (coarse_ghost[:, :, 1, :] - smoothed[:, :, -1, :])

    def faces(flux):
        reduced_terms = flux.reshape(3, groups, half, 2, P_SIZE, half, 2).mean(axis=(3, 6))
        return jnp.transpose(reduced_terms, (1, 3, 0, 2, 4)).reshape(groups, P_SIZE, 3, half * half)

    return jnp.concatenate([blocks, faces(flux_low), faces(flux_high)], axis=3)


def on_device(velocity, coarse_ghost, viscosity, stress, patch_mask, coarse_owner):
    cells_x = velocity.shape[1]
    margin = SWEEPS + 1
    stacked = with_halo(
        jnp.concatenate([velocity, stress, viscosity[None]], axis=0), (("grp", 1),), margin
    )
    ghost_ext = with_halo(coarse_ghost, (("grp", 1),), margin)
    vel_ext = stacked[:3]
    visc_ext = stacked[9]
    span = visc_ext.shape[0]
    source = KAPPA * vel_ext[:, 1:-1] + divergence(stacked[3:9])
    rows = source.shape[1]
    total_x = cells_x * lax.axis_size("grp")
    first_cell = lax.axis_index("grp") * cells_x
    for sweep_index in range(SWEEPS):
        ghost_rows = ghost_ext[:, sweep_index + 1 : span - sweep_index - 1]
        applied, diagonal = apply_operator(
            vel_ext, ghost_rows, visc_ext[sweep_index : span - sweep_index]
        )
        source_part = source[:, sweep_index : rows - sweep_index]
        patch_positions = (
            first_cell - (margin - 1 - sweep_index) + jnp.arange(applied.shape[1], dtype=jnp.int32)
        )
        inside = ((patch_positions >= 0) & (patch_positions < total_x)).astype(jnp.float32)
        interior = vel_ext[:, 1:-1]
        vel_ext = (
            interior + OMEGA * (source_part - applied) / diagonal * inside[None, :, None, None]
        )
    ghost_rows = ghost_ext[:, SWEEPS + 1 : span - SWEEPS - 1]
    applied, diagonal = apply_operator(vel_ext, ghost_rows, visc_ext[SWEEPS : span - SWEEPS])
    residual = source[:, SWEEPS : rows - SWEEPS] - applied
    smoothed = vel_ext[:, 1:-1]
    fine_patches = patch_data(residual, smoothed, viscosity, coarse_ghost, 1).reshape(
        P_SIZE, 3 * PV
    )
    fine_patches = fine_patches * patch_mask[0][:, None].astype(jnp.float32)
    owner_row = coarse_owner[0]
    row_ids = jnp.arange(lax.axis_size("wide") * CP_DEV, dtype=jnp.int32)
    indicator_matrix = (owner_row[None, :] == row_ids[:, None]).astype(jnp.float32)
    coarse = lax.psum_scatter(
        jnp.dot(indicator_matrix, fine_patches, precision=lax.Precision.HIGHEST),
        "wide",
        scatter_dimension=0,
        tiled=True,
    )
    return (smoothed, coarse.reshape(1, CP_DEV, 3, PV))


def solution(mesh):
    in_specs = (
        P(None, "grp", "wide", None),
        P(None, "grp", "wide", None),
        P("grp", "wide", None),
        P(None, "grp", "wide", None),
        P("grp", "wide"),
        P("grp", "wide"),
    )
    out_specs = (P(None, "grp", "wide", None), P("grp", "wide", None, None))
    return jax.shard_map(
        on_device, mesh=mesh, in_specs=in_specs, out_specs=out_specs, check_vma=False
    )
```

profile of v0, /device:TPU:11, one launch (start us, length us, event | category | flops | bytes accessed | tf_op | source)
XLA Modules:
  0.0 231.7 jit_solution(15209556971537715738)
XLA Ops:
  7.2 1.1 copy.157
  8.3 1.7 copy.126
  11.0 2.2 collective-permute-start.1
  13.2 4.0 %collective-permute-start = (f32[10,4,8,128]{3,1,2,0:T(4,128)}, f32[10,4,8,128]{3,1,2,0:T(4,128)S(1)}, u32[]{:S(2)}, u32[]{:S(2)}) collective-permute-start(f32[10,4,8,128]{3,1,2,0:T(4,128)} %get-tuple-element.53), channel_id=1, source_target_pairs={{0,4},{4,8},{8,12},{12,16},{16,20},{20,24},{24,28},{1,5},{5,9},{9,... | collective-permute-start | bytes 491528 | tf_op jit(solution)/shard_map/ppermute | solution.py:23
  17.9 1.9 collective-permute-start.3
  19.8 4.3 %collective-permute-start.2 = (f32[3,4,2,128]{3,1,0,2:T(4,128)}, f32[3,4,2,128]{3,1,0,2:T(4,128)}, u32[]{:S(2)}, u32[]{:S(2)}) collective-permute-start(f32[3,4,2,128]{3,1,0,2:T(4,128)} %get-tuple-element.155), channel_id=1, source_target_pairs={{0,4},{4,8},{8,12},{12,16},{16,20},{20,24},{24,28},{1,5},{5,9},{9,... | collective-permute-start | bytes 36872 | tf_op jit(solution)/shard_map/ppermute | solution.py:23
  28.9 2.5 %fusion.109 = (f32[64,8,128]{2,1,0:T(8,128)S(1)}, f32[64,8,128]{2,1,0:T(8,128)}, f32[64,8,128]{2,1,0:T(8,128)}, f32[64,8,128]{2,1,0:T(8,128)}) fusion(f32[64,8,128]{2,1,0:T(8,128)S(1)} %copy-done, f32[64,1,128]{2,1,0:T(1,128)S(1)} %get-tuple-element.141, f32[64,7,128]{2,1,0:T(8,128)} %get-tuple-element.139, f32[64,128]{1,0:T(8,128)S(1)} %bitcast.239, ...), kind=kLoop, calls=%fused_computation.210 | loop fusion | flops 917504 | bytes 2424848 | tf_op jit(solution)/shard_map/mul | solution.py:44
  31.4 4.2 %mul.571 = f32[32,2,2,32,2]{4,3,2,1,0:T(8,128)} reshape(f32[64,128]{1,0:T(8,128)} %get-tuple-element.11) | data formatting | bytes 65536 | tf_op jit(solution)/shard_map/mul | solution.py:91
  35.5 4.2 %mul.568 = f32[32,2,2,32,2]{4,3,2,1,0:T(8,128)} reshape(f32[64,128]{1,0:T(8,128)} %get-tuple-element.10) | data formatting | bytes 65536 | tf_op jit(solution)/shard_map/mul | solution.py:90
  39.8 1.7 copy.147
  41.5 1.7 copy.146
  44.7 1.0 pad_maximum_fusion.7
  49.9 1.7 multiply_add_fusion.2
  53.4 1.3 multiply_add_fusion.1
  56.6 1.3 multiply_add_fusion
  57.9 1.3 fusion.143
  59.2 1.4 fusion.140
  60.7 1.5 fusion.141
  62.9 8.4 %sub.306 = f32[3,1,32,2,2,32,2]{6,5,4,3,2,0,1:T(8,128)} reshape(f32[3,64,1,128]{3,1,2,0:T(8,128)} %get-tuple-element.61) | data formatting | bytes 196608 | tf_op jit(solution)/shard_map/sub | solution.py:91
  71.3 4.4 %multiply_reduce_fusion = f32[3,32,2,32]{3,2,1,0:T(2,128)S(1)} fusion(f32[3,1,32,2,2,32,2]{6,5,4,3,2,0,1:T(8,128)} %sub.306, f32[32,2,2,32,2]{4,3,2,1,0:T(8,128)} %mul.571), kind=kLoop, calls=%fused_computation | loop fusion | flops 43008 | bytes 155648 | tf_op jit(solution)/shard_map/reduce_sum | solution.py:94
  76.4 1.0 reshape.770
  77.4 8.4 %sub.304 = f32[3,1,32,2,2,32,2]{6,5,4,3,2,0,1:T(8,128)} reshape(f32[3,64,1,128]{3,1,2,0:T(8,128)} %get-tuple-element.60) | data formatting | bytes 196608 | tf_op jit(solution)/shard_map/sub | solution.py:90
  85.8 4.4 %multiply_reduce_fusion.1 = f32[3,32,2,32]{3,2,1,0:T(2,128)S(1)} fusion(f32[3,1,32,2,2,32,2]{6,5,4,3,2,0,1:T(8,128)} %sub.304, f32[32,2,2,32,2]{4,3,2,1,0:T(8,128)} %mul.568), kind=kLoop, calls=%fused_computation.1 | loop fusion | flops 43008 | bytes 155648 | tf_op jit(solution)/shard_map/reduce_sum | solution.py:94
  90.9 1.0 reshape.769
  93.8 3.0 %fusion.58 = f32[3,64,8,128]{3,1,2,0:T(8,128)S(1)} fusion(f32[3,66,8,128]{3,1,2,0:T(8,128)S(1)} %multiply_add_fusion, f32[3,70,8,128]{3,1,2,0:T(8,128)S(1)} %copy-done.2, f32[3,64,1,128]{3,1,2,0:T(8,128)} %get-tuple-element.62, f32[3,64,7,128]{3,1,2,0:T(8,128)} %get-tuple-element.64, f32[3,64,7,128]{3,1,2,0:T(8,128)} %get-tuple-element.63, ...), kind=kLoop, calls=%fused_computation.84 | loop fusion | flops 4915200 | bytes 8847376 | tf_op jit(solution)/shard_map/sub | solution.py:130
  97.3 51.6 %reshape.767 = f32[3,32,2,4,2,2,32,2]{7,6,5,4,3,2,1,0:T(8,128)} reshape(f32[3,64,8,128]{3,2,1,0:T(8,128)S(1)} %copy.148) | data formatting | bytes 1572864 | tf_op jit(solution)/shard_map/reshape | solution.py:86
  148.9 18.1 %reduce_sum.27 = f32[3,32,4,2,32]{4,3,2,1,0:T(2,128)S(1)} reduce(f32[3,32,2,4,2,2,32,2]{7,6,5,4,3,2,1,0:T(8,128)} %reshape.767, f32[]{:T(128)} %constant.16.clone.1), dimensions={2,4,7}, to_apply=%region_0.1 | reduce | flops 172032 | bytes 884740 | tf_op jit(solution)/shard_map/reduce_sum | solution.py:86
  167.7 4.2 %fusion.114 = f32[64,18432]{1,0:T(8,128)} fusion(f32[2,18432]{1,0:T(2,128)S(1)} %bitcast.237, f32[2]{0:T(128)S(1)} %copy-done.21, s32[2]{0:T(128)S(1)} %bitcast.240), kind=kOutput, calls=%fused_computation.239 | convolution fusion | flops 28348544 | bytes 4866064 | tf_op jit(solution)/shard_map/dot_general | solution.py:140
  172.0 1.3 copy.152
  173.3 47.8 %reduce-scatter.2.cloned.1.call-done = f32[16,18432]{1,0:T(8,128)} async-done(((f32[64,18432]{1,0:T(8,128)}), f32[16,18432]{1,0:T(8,128)}) %reduce-scatter.2.cloned.1.call-update) | async-done | bytes 1179664 | tf_op jit(solution)/shard_map/reduce_scatter | solution.py:139
  221.1 2.0 reshape.772
  223.1 1.7 copy.153
  (126 shorter events, 20.8 us)
Async XLA Ops:
  7.2 214.0 %reduce-scatter.2.cloned.1.call-start = ((), (), s32[]{:S(2)}) async-start(), calls=%async_computation.1 | async-start | bytes 5898240 | tf_op jit(solution)/shard_map/reduce_scatter | solution.py:139
  7.2 2.8 %copy-start.14 = (f32[3,64,8,128]{3,2,1,0:T(8,128)S(1)}, f32[3,64,8,128]{3,2,1,0:T(8,128)}, u32[]{:S(2)}) copy-start(f32[3,64,8,128]{3,2,1,0:T(8,128)} %param.6) | copy-start | bytes 2359300
  10.0 7.2 %copy-start.15 = (f32[3,64,2,128]{3,2,1,0:T(2,128)S(1)}, f32[3,64,2,128]{3,2,1,0:T(2,128)}, u32[]{:S(2)}) copy-start(f32[3,64,2,128]{3,2,1,0:T(2,128)} %param.7) | copy-start | bytes 589828
  10.0 15.0 %copy-start = (f32[64,8,128]{2,1,0:T(8,128)S(1)}, f32[64,8,128]{2,1,0:T(8,128)}, u32[]{:S(2)}) copy-start(f32[64,8,128]{2,1,0:T(8,128)} %param.8) | copy-start | bytes 786436
  10.2 18.2 %copy-start.22 = (s32[1,2]{1,0:T(1,128)S(1)}, s32[1,2]{1,0:T(1,128)}, u32[]{:S(2)}) copy-start(s32[1,2]{1,0:T(1,128)} %param.10) | copy-start | bytes 28
  11.0 34.7 %collective-permute-start.1 = (f32[10,4,8,128]{3,1,2,0:T(4,128)}, f32[10,4,8,128]{3,1,2,0:T(4,128)S(1)}, u32[]{:S(2)}, u32[]{:S(2)}) collective-permute-start(f32[10,4,8,128]{3,1,2,0:T(4,128)} %get-tuple-element.54), channel_id=1, source_target_pairs={{4,0},{8,4},{12,8},{16,12},{20,16},{24,20},{28,24},{5,1},{9,5},{13... | collective-permute-start | bytes 491528 | tf_op jit(solution)/shard_map/ppermute | solution.py:26
  13.2 32.6 %collective-permute-start = (f32[10,4,8,128]{3,1,2,0:T(4,128)}, f32[10,4,8,128]{3,1,2,0:T(4,128)S(1)}, u32[]{:S(2)}, u32[]{:S(2)}) collective-permute-start(f32[10,4,8,128]{3,1,2,0:T(4,128)} %get-tuple-element.53), channel_id=1, source_target_pairs={{0,4},{4,8},{8,12},{12,16},{16,20},{20,24},{24,28},{1,5},{5,9},{9,... | collective-permute-start | bytes 491528 | tf_op jit(solution)/shard_map/ppermute | solution.py:23
  17.2 11.6 %copy-start.9 = (f32[3,64,2,128]{3,1,0,2:T(8,128)}, f32[3,64,2,128]{3,1,0,2:T(8,128)S(1)}, u32[]{:S(2)}) copy-start(f32[3,64,2,128]{3,1,0,2:T(8,128)S(1)} %copy.133) | copy-start | bytes 589828
  17.9 26.8 %collective-permute-start.3 = (f32[3,4,2,128]{3,1,0,2:T(4,128)}, f32[3,4,2,128]{3,1,0,2:T(4,128)}, u32[]{:S(2)}, u32[]{:S(2)}) collective-permute-start(f32[3,4,2,128]{3,1,0,2:T(4,128)} %get-tuple-element.156), channel_id=1, source_target_pairs={{4,0},{8,4},{12,8},{16,12},{20,16},{24,20},{28,24},{5,1},{9,5},{13... | collective-permute-start | bytes 36872 | tf_op jit(solution)/shard_map/ppermute | solution.py:26
  19.8 24.9 %collective-permute-start.2 = (f32[3,4,2,128]{3,1,0,2:T(4,128)}, f32[3,4,2,128]{3,1,0,2:T(4,128)}, u32[]{:S(2)}, u32[]{:S(2)}) collective-permute-start(f32[3,4,2,128]{3,1,0,2:T(4,128)} %get-tuple-element.155), channel_id=1, source_target_pairs={{0,4},{4,8},{8,12},{12,16},{16,20},{20,24},{24,28},{1,5},{5,9},{9,... | collective-permute-start | bytes 36872 | tf_op jit(solution)/shard_map/ppermute | solution.py:23
  24.1 32.5 %copy-start.16 = (pred[8]{0:T(512)(128)(4,1)}, pred[8]{0:T(512)(128)(4,1)S(1)}, u32[]{:S(2)}) copy-start(pred[8]{0:T(512)(128)(4,1)S(1)} %get-tuple-element.167) | copy-start | bytes 28
  24.1 32.5 %copy-start.18 = (pred[8]{0:T(512)(128)(4,1)}, pred[8]{0:T(512)(128)(4,1)S(1)}, u32[]{:S(2)}) copy-start(pred[8]{0:T(512)(128)(4,1)S(1)} %get-tuple-element.168) | copy-start | bytes 28
  31.3 11.8 %copy-start.8 = (f32[64,8,128]{2,1,0:T(8,128)S(1)}, f32[64,8,128]{2,1,0:T(8,128)}, u32[]{:S(2)}) copy-start(f32[64,8,128]{2,1,0:T(8,128)} %get-tuple-element.137) | copy-start | bytes 786436
  45.8 10.4 %copy-start.6 = (f32[10,4,8,128]{3,1,2,0:T(4,128)}, f32[10,4,8,128]{3,1,2,0:T(4,128)S(1)}, u32[]{:S(2)}) copy-start(f32[10,4,8,128]{3,1,2,0:T(4,128)S(1)} %collective-permute-done.1) | copy-start | bytes 491524
  45.8 10.4 %copy-start.7 = (f32[10,4,8,128]{3,1,2,0:T(4,128)}, f32[10,4,8,128]{3,1,2,0:T(4,128)S(1)}, u32[]{:S(2)}) copy-start(f32[10,4,8,128]{3,1,2,0:T(4,128)S(1)} %collective-permute-done) | copy-start | bytes 491524
  51.6 5.0 %copy-start.1 = (f32[3,70,8,128]{3,1,2,0:T(8,128)}, f32[3,70,8,128]{3,1,2,0:T(8,128)S(1)}, u32[]{:S(2)}) copy-start(f32[3,70,8,128]{3,1,2,0:T(8,128)S(1)} %get-tuple-element.16) | copy-start | bytes 2580484
  59.2 2.9 %copy-start.10 = (f32[3,64,1,128]{3,2,1,0:T(1,128)S(1)}, f32[3,64,1,128]{3,2,1,0:T(1,128)}, u32[]{:S(2)}) copy-start(f32[3,64,1,128]{3,2,1,0:T(1,128)} %get-tuple-element.153) | copy-start | bytes 294916
  59.2 2.9 %copy-start.12 = (f32[3,64,1,128]{3,2,1,0:T(1,128)S(1)}, f32[3,64,1,128]{3,2,1,0:T(1,128)}, u32[]{:S(2)}) copy-start(f32[3,64,1,128]{3,2,1,0:T(1,128)} %get-tuple-element.154) | copy-start | bytes 294916
  91.9 1.2 copy-start.2
  91.9 1.4 copy-start.3
  91.9 1.6 copy-start.4
  91.9 1.9 copy-start.5
  91.9 1.8 copy-start.11
  91.9 1.9 copy-start.13
  91.9 1.9 copy-start.17
  91.9 1.8 copy-start.19
  148.9 18.8 %copy-start.20 = (s32[1,2]{1,0:T(1,128)S(1)}, s32[1,2]{1,0:T(1,128)}, u32[]{:S(2)}) copy-start(s32[1,2]{1,0:T(1,128)} %param.11) | copy-start | bytes 28
  148.9 18.8 %copy-start.21 = (f32[2]{0:T(128)S(1)}, f32[2]{0:T(128)}, u32[]{:S(2)}) copy-start(f32[2]{0:T(128)} %convert_bitcast_fusion) | copy-start | bytes 28
Sparse Core Ops, SparseCore 0:
  172.0 49.0 reduce-scatter.1
where the time goes:
time: 234 us; the launch traced here: 232 us
  local copies, waits for them, and re-layouts  108 us (46%)
  waiting for transfers between devices  47.8 us (20%)
  other arithmetic  44.4 us (19%)
  between operations  14.8 us (6%)
  starting transfers between devices  12.4 us (5%)
  matrix products  4.21 us (2%)
    reshape x1, local copies, waits for them, and re-layouts, patch_data(): residual.reshape(3, groups, half, 2, CY // 2, 2, P_SIZE, half, 2)  51.6 us
    reduce_scatter x1, waiting for transfers between devices, on_device(): lax.psum_scatter(jnp.dot(indicator_matrix, fine_patches, precision=lax.Pr...  47.8 us
    reduce_sum x1, other arithmetic, patch_data(): residual.reshape(3, groups, half, 2, CY // 2, 2, P_SIZE, half, 2)  18.1 us
    reduce_sum x2, other arithmetic, faces(): flux.reshape(3, groups, half, 2, P_SIZE, half, 2).mean(axis=(3, 6))  8.72 us
    sub x1, local copies, waits for them, and re-layouts, patch_data(): smoothed[:, :, 0, :] - coarse_ghost[:, :, 0, :]  8.41 us
    sub x1, local copies, waits for them, and re-layouts, patch_data(): coarse_ghost[:, :, 1, :] - smoothed[:, :, -1, :]  8.41 us
    ppermute x2, starting transfers between devices, with_halo(): lax.ppermute(lax.slice_in_dim(block, block.shape[dim] - width, None, axis...  8.28 us
    unnamed x52, local copies, waits for them, and re-layouts  6.91 us
  transfers between devices with their start and end apart: 5, of which 1 were waited for; matrix products, arithmetic and copies ran while one was open for 10% of the time, Pallas kernels for 0%

commit v1 on v0

v1 whole, which is shorter than its diff:
```python
import functools

import jax
import jax.numpy as jnp
import numpy as np
from jax import lax
from jax.experimental import pallas as pl
from jax.experimental.pallas import tpu as pltpu
from jax.sharding import PartitionSpec as P

PATCH = 64
CY = 8
P_SIZE = 2
CP_DEV = 16
SWEEPS = 3
PV = 6144

KAPPA = 1.0
OMEGA = 0.8

R_U = 0
R_V = 96
R_F = 128
R_S = 200
R_G = 224
PACK = 248

T_U = 0
T_C = 18
T_G = 39
STATE = 48

HALF = PATCH // 2
ROWS_C = HALF + 2 * (HALF // 4)
SLOT = 3 * ROWS_C + 8
UNROLL = 10


def pool_matrix(cz):
    k = np.arange(4 * cz)[:, None]
    n = np.arange(P_SIZE * cz)[None, :]
    same_row = (k // cz) == (n % cz) // HALF
    same_col = (k % cz) // 2 == (n // cz) * HALF + n % HALF
    return (same_row & same_col).astype(np.float32)


def up_z(v):
    return pltpu.roll(v, v.shape[1] - 1, 1)


def down_z(v):
    return pltpu.roll(v, 1, 1)


def north_of(v, high):
    row = lax.broadcasted_iota(jnp.int32, v.shape, 0)
    return jnp.where(row == CY - 1, high, pltpu.roll(v, CY - 1, 0))


def south_of(v, low):
    row = lax.broadcasted_iota(jnp.int32, v.shape, 0)
    return jnp.where(row == 0, low, pltpu.roll(v, 1, 0))


def edge_rows(v):
    row = lax.broadcasted_iota(jnp.int32, v.shape, 0)
    north = jnp.where(row == CY - 1, v, pltpu.roll(v, CY - 1, 0))
    south = jnp.where(row == 0, v, pltpu.roll(v, 1, 0))
    return north, south


def diff_y(v):
    row = lax.broadcasted_iota(jnp.int32, v.shape, 0)
    north = jnp.where(row == CY - 1, 0.0, pltpu.roll(v, CY - 1, 0))
    south = jnp.where(row == 0, 0.0, pltpu.roll(v, 1, 0))
    return north - south


def diff_z(v):
    return up_z(v) - down_z(v)


def coefficients(v, v_west, v_east):
    v_north, v_south = edge_rows(v)
    half = 0.5 * v
    east = half + 0.5 * v_east
    west = half + 0.5 * v_west
    north = half + 0.5 * v_north
    south = half + 0.5 * v_south
    up = half + 0.5 * up_z(v)
    down = down_z(up)
    diagonal = KAPPA + ((east + west) + (north + south)) + (up + down)
    scale = OMEGA / diagonal
    return (
        [scale * west, scale * east, scale * south, scale * north, scale * down, scale * up],
        diagonal * (1.0 / OMEGA),
        scale,
    )


def gather_terms(g, c, u, u_west, u_east, low, high):
    x = c[0] * u_west + c[1] * u_east
    y = c[2] * south_of(u, low) + c[3] * north_of(u, high)
    z = c[4] * down_z(u) + c[5] * up_z(u)
    return (g + x) + (y + z)


def pack_kernel(vel, ghost, visc, stress, out_a, out_b, u_s, v_s, s_s, g_s, sem):
    rows = vel.shape[1]
    copies = []
    for side in range(2):
        r0 = 0 if side == 0 else rows - 4 * CY
        g0 = 0 if side == 0 else ghost.shape[1] - 8
        for n, (src, dst) in enumerate(
            (
                (stress.at[:, pl.ds(r0, 4 * CY)], s_s.at[side]),
                (vel.at[:, pl.ds(r0, 4 * CY)], u_s.at[side]),
                (visc.at[pl.ds(r0, 4 * CY)], v_s.at[side]),
                (ghost.at[:, pl.ds(g0, 8)], g_s.at[side]),
            )
        ):
            copies.append(pltpu.make_async_copy(src, dst, sem.at[side, n]))
    for c in copies:
        c.start()
    for c in copies:
        c.wait()
    even = lax.axis_index("grp") % 2 == 0

    def plane(ref, side, comp, p):
        return ref[side, comp, p * CY : (p + 1) * CY, :]

    packs = []
    for side in range(2):
        parts = {}
        for c in range(3):
            parts[R_U + c * 32] = u_s[side, c]
        parts[R_V] = v_s[side]
        for j in range(3):
            p = j if side == 0 else j + 1

            def dx(comp):
                if p == 0:
                    return plane(s_s, side, comp, p + 1)
                if p == 3:
                    return -plane(s_s, side, comp, p - 1)
                return plane(s_s, side, comp, p + 1) - plane(s_s, side, comp, p - 1)

            xx, yy, zz, xy, xz, yz = range(6)
            s_xy, s_xz, s_yz = (plane(s_s, side, k, p) for k in (xy, xz, yz))
            s_yy, s_zz = (plane(s_s, side, k, p) for k in (yy, zz))
            f = (
                dx(xx) + diff_y(s_xy) + diff_z(s_xz),
                dx(xy) + diff_y(s_yy) + diff_z(s_yz),
                dx(xz) + diff_y(s_yz) + diff_z(s_zz),
            )
            for c in range(3):
                parts[R_F + (c * 3 + j) * CY] = KAPPA * plane(u_s, side, c, p) + 0.5 * f[c]
        edge = 0 if side == 0 else 3
        for c, k in enumerate((xx, xy, xz)):
            parts[R_S + c * CY] = plane(s_s, side, k, edge)
        for c in range(3):
            parts[R_G + c * 8] = g_s[side, c]
        packs.append(parts)
    for r, low in packs[0].items():
        high = packs[1][r]
        out_a[r : r + low.shape[0], :] = jnp.where(even, high, low)
        out_b[r : r + low.shape[0], :] = jnp.where(even, low, high)


def split_dot(x, m):
    hi = x.astype(jnp.bfloat16)
    rest = x - hi.astype(jnp.float32)
    mid = rest.astype(jnp.bfloat16)
    lo = (rest - mid.astype(jnp.float32)).astype(jnp.bfloat16)
    dot = functools.partial(jnp.dot, preferred_element_type=jnp.float32)
    return dot(hi, m) + (dot(mid, m) + dot(lo, m))


def over_planes(first, last, unroll, body):
    steps = (last - first) // unroll

    def step(t, _):
        for j in range(unroll):
            body(first + t * unroll + j)
        return 0

    lax.fori_loop(0, steps, step, 0)
    for i in range(first + steps * unroll, last):
        body(i)


def interior_kernel(
    vel, ghost, visc, stress, pool, new_v, state, pooled, coef, gsrc, ua, ub, s_sum, flux, xmat
):
    planes = visc.shape[0] // CY
    cz = visc.shape[1]

    def at(i):
        return pl.ds(i * CY if isinstance(i, int) else pl.multiple_of(i * CY, CY), CY)

    def ghosts(c, i):
        return ghost[c, pl.ds(2 * i, 1), :], ghost[c, pl.ds(2 * i + 1, 1), :]

    def first(i):
        c, diag, scale = coefficients(visc[at(i)], visc[at(i - 1)], visc[at(i + 1)])
        for k in range(6):
            coef[k, at(i)] = c[k]
        coef[6, at(i)] = diag

        def dx(k):
            return stress[k, at(i + 1)] - stress[k, at(i - 1)]

        s_xy, s_xz, s_yz = (stress[k, at(i)] for k in (3, 4, 5))
        f = (
            dx(0) + diff_y(s_xy) + diff_z(s_xz),
            dx(3) + diff_y(stress[1, at(i)]) + diff_z(s_yz),
            dx(4) + diff_y(s_yz) + diff_z(stress[2, at(i)]),
        )
        for k in range(3):
            u = vel[k, at(i)]
            g = scale * (KAPPA * u + 0.5 * f[k])
            gsrc[k, at(i)] = g
            low, high = ghosts(k, i)
            t = gather_terms(g, c, u, vel[k, at(i - 1)], vel[k, at(i + 1)], low, high)
            ua[k, at(i)] = (1.0 - OMEGA) * u + t

    over_planes(1, planes - 1, UNROLL, first)

    def sweep(src, dst):
        def body(i):
            c = [coef[k, at(i)] for k in range(6)]
            for k in range(3):
                u = src[k, at(i)]
                low, high = ghosts(k, i)
                t = gather_terms(
                    gsrc[k, at(i)], c, u, src[k, at(i - 1)], src[k, at(i + 1)], low, high
                )
                dst[k, at(i)] = (1.0 - OMEGA) * u + t

        return body

    over_planes(2, planes - 2, UNROLL, sweep(ua, ub))
    over_planes(3, planes - 3, UNROLL, sweep(ub, new_v))

    s_sum[...] = jnp.zeros_like(s_sum)

    def residuals(b):
        for k in range(3):
            total = None
            for j in range(2):
                i = 2 * b + j
                c = [coef[n, at(i)] for n in range(6)]
                u = new_v[k, at(i)]
                low, high = ghosts(k, i)
                t = gather_terms(
                    gsrc[k, at(i)], c, u, new_v[k, at(i - 1)], new_v[k, at(i + 1)], low, high
                )
                r = (t - OMEGA * u) * coef[6, at(i)]
                total = r if total is None else total + r
            s_sum[k, at(b)] = total

    over_planes(2, planes // 2 - 2, UNROLL // 2, residuals)

    keep = lax.broadcasted_iota(jnp.int32, (planes, cz), 0)
    keep = (keep >= SWEEPS) & (keep < planes - SWEEPS)
    for k in range(3):
        for face in range(2):
            row = 0 if face == 0 else CY - 1
            nu = visc[pl.ds(row, planes, stride=CY), :]
            cell = new_v[k, pl.ds(row, planes, stride=CY), :]
            outer = ghost[k, pl.ds(face, planes, stride=2), :]
            value = nu * (cell - outer) if face == 0 else nu * (outer - cell)
            flux[...] = jnp.where(keep, value, 0.0)
            for j in range(4):
                both = flux[pl.ds(2 * j, planes // 8, stride=8), :] + flux[
                    pl.ds(2 * j + 1, planes // 8, stride=8), :
                ]
                base = k * ROWS_C + HALF + face * (HALF // 4)
                xmat[base : base + HALF // 4, j * cz : (j + 1) * cz] = 0.25 * both
        for j in range(4):
            both = s_sum[k, pl.ds(2 * j, planes // 2, stride=CY), :] + s_sum[
                k, pl.ds(2 * j + 1, planes // 2, stride=CY), :
            ]
            xmat[k * ROWS_C : k * ROWS_C + HALF, j * cz : (j + 1) * cz] = 0.125 * both
    pooled[...] = split_dot(xmat[...], pool[...])

    for side in range(2):

        def depth(d):
            i = d if side == 0 else planes - 1 - d
            return slice(i * CY, (i + 1) * CY)

        def put(n, value):
            state[side, n * CY : (n + 1) * CY, :] = value

        for s, ref in ((1, ua), (2, ub), (3, new_v)):
            for k in range(3):
                for e in range(2):
                    put(T_U + (s - 1) * 6 + k * 2 + e, ref[k, depth(s + e), :])
        for d in range(1, 4):
            for n in range(7):
                put(T_C + n * 3 + d - 1, coef[n, depth(d), :])
            for k in range(3):
                put(T_G + k * 3 + d - 1, gsrc[k, depth(d), :])


def edge_kernel(
    n_wide,
    owner,
    mask,
    in_a,
    in_b,
    got_a,
    got_b,
    state,
    pooled,
    pool,
    velocity_in,
    velocity_out,
    *refs,
):
    slots = refs[:n_wide]
    u_out, xmat, flux, total_s, out_sem = refs[n_wide:]
    del velocity_in
    grp = lax.axis_index("grp")
    even = grp % 2 == 0
    ends = (grp > 0, grp < lax.axis_size("grp") - 1)

    cz = pool.shape[0] // 4
    xmat[...] = jnp.zeros_like(xmat)
    flux[...] = jnp.zeros_like(flux)
    for side in range(2):
        sign = -1.0 if side == 0 else 1.0
        inside = jnp.where(ends[side], 1.0, 0.0)

        def index(q, count):
            if q >= 0:
                return q if side == 0 else count - 1 - q
            return count + q if side == 0 else -q - 1

        def get(q, start, comp, count, rows=CY):
            r = start + (comp * count + index(q, count)) * rows
            return packed(q >= 0, r, rows)

        def packed(own, r, rows=CY):
            a, b = (in_a, in_b) if own else (got_a, got_b)
            a, b = a[r : r + rows, :], b[r : r + rows, :]
            return jnp.where(even, b, a) if side == 0 else jnp.where(even, a, b)

        def saved(n):
            return state[side, n * CY : (n + 1) * CY, :]

        visc = {q: get(q, R_V, 0, 4) for q in range(-4, 2)}
        ghost = {
            (k, q): get(q, R_G, k, 4, 2) for k in range(3) for q in range(-3, 4)
        }
        coef, diag, g = {}, {}, {}
        for q in range(-3, 1):
            c, d, scale = coefficients(visc[q], visc[q - 1], visc[q + 1])
            coef[q], diag[q] = c, d
            for k in range(3):
                f = get(q, R_F, k, 3)
                if q == 0:
                    f = f + (0.5 * sign) * packed(False, R_S + k * CY)
                if q == -1:
                    f = f - (0.5 * sign) * packed(True, R_S + k * CY)
                g[k, q] = scale * f
        for q in range(1, 4):
            c = [saved(T_C + n * 3 + q - 1) for n in range(7)]
            coef[q], diag[q] = ([c[0], c[1]] if side == 0 else [c[1], c[0]]) + c[2:6], c[6]
            for k in range(3):
                g[k, q] = saved(T_G + k * 3 + q - 1)
        for k in range(3):
            u = {q: get(q, R_U, k, 4) for q in range(-4, 2)}
            for s in range(1, SWEEPS + 1):
                new = {}
                for q in range(s - 4, s):
                    low, high = ghost[k, q][0:1], ghost[k, q][1:2]
                    t = gather_terms(g[k, q], coef[q], u[q], u[q - 1], u[q + 1], low, high)
                    value = (1.0 - OMEGA) * u[q] + t
                    new[q] = value * inside if q < 0 else value
                for e in range(2):
                    new[s + e] = saved(T_U + (s - 1) * 6 + k * 2 + e)
                u = new
            for q in range(3):
                i = q if side == 0 else 2 - q
                u_out[side, k, i * CY : (i + 1) * CY, :] = u[q]
            sums = []
            for b in range(2):
                total = None
                for q in (2 * b, 2 * b + 1):
                    low, high = ghost[k, q][0:1], ghost[k, q][1:2]
                    t = gather_terms(g[k, q], coef[q], u[q], u[q - 1], u[q + 1], low, high)
                    r = (t - OMEGA * u[q]) * diag[q]
                    total = r if total is None else total + r
                sums.append(total)
            for b in range(2):
                row = b if side == 0 else 3 - b
                both = sums[b] + pltpu.roll(sums[b], CY - 1, 0)
                for j in range(4):
                    xmat[k * 8 + row : k * 8 + row + 1, j * cz : (j + 1) * cz] = (
                        0.125 * both[2 * j : 2 * j + 1, :]
                    )
            for q in range(3):
                x = q if side == 0 else 7 - q
                nu = get(q, R_V, 0, 4)
                low, high = ghost[k, q][0:1], ghost[k, q][1:2]
                flux[side, k, 0, x : x + 1, :] = nu[0:1] * (u[q][0:1] - low)
                flux[side, k, 1, x : x + 1, :] = nu[CY - 1 :] * (high - u[q][CY - 1 :])
            for face in range(2):
                for j in range(4):
                    row = k * 8 + 4 + face * 2 + side
                    xmat[row : row + 1, j * cz : (j + 1) * cz] = 0.25 * (
                        flux[side, k, face, 2 * j : 2 * j + 1, :]
                        + flux[side, k, face, 2 * j + 1 : 2 * j + 2, :]
                    )
    rows = velocity_out.shape[1]
    out_copies = [
        pltpu.make_async_copy(
            u_out.at[side],
            velocity_out.at[:, pl.ds(0 if side == 0 else rows - 3 * CY, 3 * CY)],
            out_sem.at[side],
        )
        for side in range(2)
    ]
    for c in out_copies:
        c.start()

    edge = split_dot(xmat[...], pool[...])
    places = (0, 1, HALF - 2, HALF - 1, HALF, HALF + HALF // 4 - 1, HALF + HALF // 4, ROWS_C - 1)
    total_s[...] = pooled[...]
    for k in range(3):
        for n, place in enumerate(places):
            r = k * ROWS_C + place
            total_s[r : r + 1, :] = total_s[r : r + 1, :] + edge[k * 8 + n : k * 8 + n + 1, :]
    me = lax.axis_index("wide")
    for d in range(n_wide):
        value, local = None, jnp.float32(-1.0)
        for p in range(P_SIZE):
            match = owner[0, p] // CP_DEV == me ^ d
            weight = jnp.where(match, mask[0, p], 0).astype(jnp.float32)
            local = jnp.where(match, (owner[0, p] % CP_DEV).astype(jnp.float32), local)
            term = total_s[:, p * cz : (p + 1) * cz] * weight
            value = term if value is None else value + term
        slots[d][0 : 3 * ROWS_C, :] = value
        slots[d][3 * ROWS_C :, :] = jnp.full((8, cz), local, jnp.float32)
    for c in out_copies:
        c.wait()


def collect_kernel(n_wide, *refs):
    slots, out = refs[:n_wide], refs[n_wide]
    cz = slots[0].shape[1]
    rows = lax.broadcasted_iota(jnp.int32, (CP_DEV, cz), 0).astype(jnp.float32)
    takes = [rows == slot[3 * ROWS_C : 3 * ROWS_C + 1, :] for slot in slots]
    for k in range(3):
        for n in range(ROWS_C):
            total = None
            for take, slot in zip(takes, slots, strict=True):
                r = k * ROWS_C + n
                term = jnp.where(take, slot[r : r + 1, :], 0.0)
                total = term if total is None else total + term
            out[k, :, n * cz : (n + 1) * cz] = total


def on_device(velocity, coarse_ghost, viscosity, stress, patch_mask, coarse_owner):
    n_grp, n_wide = lax.axis_size("grp"), lax.axis_size("wide")
    cells_x, cz = viscosity.shape[0], viscosity.shape[2]
    f32 = jnp.float32
    vel = velocity.reshape(3, cells_x * CY, cz)
    ghost = coarse_ghost.reshape(3, cells_x * 2, cz)
    visc = viscosity.reshape(cells_x * CY, cz)
    strs = stress.reshape(6, cells_x * CY, cz)
    pool = jnp.asarray(pool_matrix(cz), jnp.bfloat16)

    anywhere = pl.BlockSpec(memory_space=pl.ANY)
    vmem = pl.BlockSpec(memory_space=pltpu.VMEM)
    smem = pl.BlockSpec(memory_space=pltpu.SMEM)
    pack_shape = jax.ShapeDtypeStruct((PACK, cz), f32)
    pack_a, pack_b = pl.pallas_call(
        pack_kernel,
        out_shape=(pack_shape, pack_shape),
        in_specs=[anywhere] * 4,
        out_specs=(vmem, vmem),
        scratch_shapes=[
            pltpu.VMEM((2, 3, 4 * CY, cz), f32),
            pltpu.VMEM((2, 4 * CY, cz), f32),
            pltpu.VMEM((2, 6, 4 * CY, cz), f32),
            pltpu.VMEM((2, 3, 8, cz), f32),
            pltpu.SemaphoreType.DMA((2, 4)),
        ],
        name="pack",
    )(vel, ghost, visc, strs)

    pairs_a = [(i, i ^ 1) for i in range(n_grp) if i ^ 1 < n_grp]
    pairs_b = [(i, j) for i in range(n_grp) for j in [((i + 1) ^ 1) - 1] if 0 <= j < n_grp]
    got_b = lax.ppermute(pack_b, "grp", pairs_b)
    got_a = lax.ppermute(pack_a, "grp", pairs_a)

    rows = cells_x * CY
    new_v, state, pooled = pl.pallas_call(
        interior_kernel,
        out_shape=(
            jax.ShapeDtypeStruct((3, rows, cz), f32),
            jax.ShapeDtypeStruct((2, STATE * CY, cz), f32),
            jax.ShapeDtypeStruct((3 * ROWS_C, P_SIZE * cz), f32),
        ),
        in_specs=[vmem] * 5,
        out_specs=(vmem, vmem, vmem),
        scratch_shapes=[
            pltpu.VMEM((7, rows, cz), f32),
            pltpu.VMEM((3, rows, cz), f32),
            pltpu.VMEM((3, rows, cz), f32),
            pltpu.VMEM((3, rows, cz), f32),
            pltpu.VMEM((3, rows // 2, cz), f32),
            pltpu.VMEM((cells_x, cz), f32),
            pltpu.VMEM((3 * ROWS_C, 4 * cz), f32),
        ],
        cost_estimate=pl.CostEstimate(flops=100_000_000, bytes_accessed=4_000_000, transcendentals=0),
        name="interior",
    )(vel, ghost, visc, strs, pool)

    slot_shape = jax.ShapeDtypeStruct((SLOT, cz), f32)
    outs = pl.pallas_call(
        functools.partial(edge_kernel, n_wide),
        out_shape=(jax.ShapeDtypeStruct(new_v.shape, f32),) + (slot_shape,) * n_wide,
        in_specs=[smem, smem] + [vmem] * 7 + [anywhere],
        out_specs=(anywhere,) + (vmem,) * n_wide,
        scratch_shapes=[
            pltpu.VMEM((2, 3, 3 * CY, cz), f32),
            pltpu.VMEM((24, 4 * cz), f32),
            pltpu.VMEM((2, 3, 2, 8, cz), f32),
            pltpu.VMEM((3 * ROWS_C, P_SIZE * cz), f32),
            pltpu.SemaphoreType.DMA((2,)),
        ],
        input_output_aliases={9: 0},
        name="edge",
    )(coarse_owner, patch_mask, pack_a, pack_b, got_a, got_b, state, pooled, pool, new_v)
    smoothed, slots = outs[0], list(outs[1:])

    for k in range(1, n_wide):
        slots[k] = lax.ppermute(slots[k], "wide", [(i, i ^ k) for i in range(n_wide)])
    coarse = pl.pallas_call(
        functools.partial(collect_kernel, n_wide),
        out_shape=jax.ShapeDtypeStruct((3, CP_DEV, PV), f32),
        in_specs=[vmem] * n_wide,
        out_specs=vmem,
        name="collect",
    )(*slots)
    return smoothed.reshape(velocity.shape), coarse.transpose(1, 0, 2)[None]


def solution(mesh):
    in_specs = (
        P(None, "grp", "wide", None),
        P(None, "grp", "wide", None),
        P("grp", "wide", None),
        P(None, "grp", "wide", None),
        P("grp", "wide"),
        P("grp", "wide"),
    )
    out_specs = (P(None, "grp", "wide", None), P("grp", "wide", None, None))
    return jax.shard_map(
        on_device, mesh=mesh, in_specs=in_specs, out_specs=out_specs, check_vma=False
    )
```

time: 234 us -> 28.9 us (0.12)
  local copies, waits for them, and re-layouts: 108 us -> 1.3 us
  other arithmetic: 44.4 us -> 0 us
  waiting for transfers between devices: 47.8 us -> 4.36 us
  Pallas kernels: 0 us -> 14.9 us
  between operations: 14.8 us -> 0.67 us
  starting transfers between devices: 12.4 us -> 7.45 us
  matrix products: 4.21 us -> 0 us
    reshape x5 -> x0, local copies, waits for them, and re-layouts: 55.9 us -> none  [the longest x1 51.6 us: patch_data(): residual.reshape(3, groups, half, 2, CY // 2, 2, P_SIZE, half, 2)]
    reduce_scatter x1 -> x0, waiting for transfers between devices: 47.8 us -> none  [on_device(): lax.psum_scatter(jnp.dot(indicator_matrix, fine_patches, precision=lax.Pr...]
    reduce_sum x3 -> x0, other arithmetic: 26.8 us -> none  [the longest x1 18.1 us: patch_data(): residual.reshape(3, groups, half, 2, CY // 2, 2, P_SIZE, half, 2)]
    sub x3 -> x0, local copies, waits for them, and re-layouts: 17.3 us -> none  [the longest x1 8.41 us: patch_data(): smoothed[:, :, 0, :] - coarse_ghost[:, :, 0, :]]
    pallas_call x0 -> x4, Pallas kernels: none -> 14.9 us  [the longest x1 7.4 us: on_device(): pl.pallas_call(interior_kernel, out_shape=(jax.ShapeDtypeStruct((3, rows,...]
    mul x6 -> x0, local copies, waits for them, and re-layouts: 13.3 us -> none  [the longest x1 4.22 us: patch_data(): viscosity[:, 0, :] * (smoothed[:, :, 0, :] - coarse_ghost[:, :, 0, :])]
    slice x24 -> x0, local copies, waits for them, and re-layouts: 11.3 us -> none  [the longest x2 2.94 us: apply_operator(): jnp.roll(interior, 1, axis=3)]
    unnamed x52 -> x10, local copies, waits for them, and re-layouts: 6.91 us -> 1.3 us
  transfers between devices with their start and end apart: 5 -> 5, of which waited for: 1 -> 2; matrix products, arithmetic and copies ran while one was open for 10% -> 0% of each run, Pallas kernels for 0% -> 26%
where the time goes in v1:
time: 28.9 us; the launch traced here: 28.7 us
  Pallas kernels  14.9 us (52%)
  starting transfers between devices  7.45 us (26%)
  waiting for transfers between devices  4.36 us (15%)
  local copies, waits for them, and re-layouts  1.3 us (4%)
  between operations  0.67 us (2%)
    pallas_call x1, Pallas kernels, on_device(): pl.pallas_call(interior_kernel, out_shape=(jax.ShapeDtypeStruct((3, rows,...  7.4 us
    ppermute x3, waiting for transfers between devices, on_device(): lax.ppermute(slots[k], 'wide', [(i, i ^ k) for i in range(n_wide)])  4.35 us
    ppermute x1, starting transfers between devices, on_device(): got_b = lax.ppermute(pack_b, 'grp', pairs_b)  4.12 us
    pallas_call x1, Pallas kernels, on_device(): pl.pallas_call(functools.partial(edge_kernel, n_wide), out_shape=(jax.Sha...  3.3 us
    ppermute x3, starting transfers between devices, on_device(): lax.ppermute(slots[k], 'wide', [(i, i ^ k) for i in range(n_wide)])  3.01 us
    pallas_call x1, Pallas kernels, on_device(): pl.pallas_call(functools.partial(collect_kernel, n_wide), out_shape=jax.S...  2.28 us
    pallas_call x1, Pallas kernels, on_device(): pl.pallas_call(pack_kernel, out_shape=(pack_shape, pack_shape), in_specs=...  1.89 us
    unnamed x10, local copies, waits for them, and re-layouts  1.3 us
  transfers between devices with their start and end apart: 5, of which 2 were waited for; matrix products, arithmetic and copies ran while one was open for 0% of the time, Pallas kernels for 26%

profile of v1, /device:TPU:11, one launch (start us, length us, event | category | flops | bytes accessed | tf_op | source)
XLA Modules:
  0.0 28.7 jit_solution(4837926827337230340)
XLA Ops:
  0.6 1.9 %pack.1 = (f32[248,128]{1,0:T(8,128)}, f32[248,128]{1,0:T(8,128)}) custom-call(f32[3,512,128]{2,1,0:T(8,128)} %bitcast.10, f32[3,128,128]{2,1,0:T(8,128)} %bitcast.16, f32[512,128]{1,0:T(8,128)} %bitcast.13, f32[6,512,128]{2,1,0:T(8,128)} %bitcast.8), custom_call_target="tpu_custom_call" | custom-call | tf_op jit(solution)/shard_map/pack/pallas_call | solution.py:480
  2.5 0.3 %collective-permute-start = (f32[248,128]{1,0:T(8,128)}, f32[248,128]{1,0:T(8,128)S(1)}, u32[]{:S(2)}, u32[]{:S(2)}) collective-permute-start(f32[248,128]{1,0:T(8,128)} %get-tuple-element.12.in_a), channel_id=1, source_target_pairs={{0,4},{4,0},{8,12},{12,8},{16,20},{20,16},{24,28},{28,24},{1,5},{5... | collective-permute-start | bytes 380936 | tf_op jit(solution)/shard_map/ppermute | solution.py:498
  2.8 4.1 %collective-permute-start.1 = (f32[248,128]{1,0:T(8,128)}, f32[248,128]{1,0:T(8,128)S(1)}, u32[]{:S(2)}, u32[]{:S(2)}) collective-permute-start(f32[248,128]{1,0:T(8,128)} %get-tuple-element.13.in_b), channel_id=1, source_target_pairs={{4,8},{8,4},{12,16},{16,12},{20,24},{24,20},{5,9},{9,5},{13,17},{1... | collective-permute-start | bytes 380936 | tf_op jit(solution)/shard_map/ppermute | solution.py:497
  7.0 7.4 %interior.1 = (f32[3,512,128]{2,1,0:T(8,128)}, f32[2,384,128]{2,1,0:T(8,128)}, f32[144,256]{1,0:T(8,128)}) custom-call(f32[3,512,128]{2,1,0:T(8,128)} %bitcast.11, f32[3,128,128]{2,1,0:T(8,128)} %bitcast.17, f32[512,128]{1,0:T(8,128)} %bitcast.14, f32[6,512,128]{2,1,0:T(8,128)} %bitcast.9, bf16[512,256]{1,0:T(8,128)(2,1)} %constant.2.clone.pool), custom_call_target="tpu_custom_call" | custom-call | flops 100000000 | bytes 4000000 | tf_op jit(solution)/shard_map/interior/pallas_call | solution.py:501
  14.4 0.0 collective-permute-done.got_a
  14.4 0.0 copy-start
  14.4 0.0 collective-permute-done.1.got_b
  14.4 0.0 copy-start.1
  14.4 0.6 %copy-done = f32[248,128]{1,0:T(8,128)} copy-done((f32[248,128]{1,0:T(8,128)}, f32[248,128]{1,0:T(8,128)S(1)}, u32[]{:S(2)}) %copy-start) | copy-done | bytes 127000
  15.0 0.0 copy-done.1
  15.1 3.3 %edge.1 = (f32[3,512,128]{2,1,0:T(8,128)}, f32[152,128]{1,0:T(8,128)}, f32[152,128]{1,0:T(8,128)}, f32[152,128]{1,0:T(8,128)}, f32[152,128]{1,0:T(8,128)}) custom-call(s32[1,2]{1,0:T(1,128)} %owner.1, s32[1,2]{1,0:T(1,128)} %mask.1, f32[248,128]{1,0:T(8,128)} %get-tuple-element.12.in_a, ...), custom_call_target="tpu_custom_call", output_to_operand_aliasing={{0}: (9, {})} | custom-call | tf_op jit(solution)/shard_map/edge/pallas_call | solution.py:524
  18.4 1.3 %collective-permute-start.2 = (f32[152,128]{1,0:T(8,128)}, f32[152,128]{1,0:T(8,128)S(1)}, u32[]{:S(2)}, u32[]{:S(2)}) collective-permute-start(f32[152,128]{1,0:T(8,128)} %get-tuple-element.19), channel_id=1, source_target_pairs={{0,1},{1,0},{2,3},{3,2},{4,5},{5,4},{6,7},{7,6},{8,9},{9,8},{10,11... | collective-permute-start | bytes 233480 | tf_op jit(solution)/shard_map/ppermute | solution.py:542
  19.7 1.2 %collective-permute-start.3 = (f32[152,128]{1,0:T(8,128)}, f32[152,128]{1,0:T(8,128)S(1)}, u32[]{:S(2)}, u32[]{:S(2)}) collective-permute-start(f32[152,128]{1,0:T(8,128)} %get-tuple-element.20), channel_id=1, source_target_pairs={{0,2},{1,3},{2,0},{3,1},{4,6},{5,7},{6,4},{7,5},{8,10},{9,11},{10,... | collective-permute-start | bytes 233480 | tf_op jit(solution)/shard_map/ppermute | solution.py:542
  20.9 0.5 %collective-permute-start.4 = (f32[152,128]{1,0:T(8,128)}, f32[152,128]{1,0:T(8,128)S(1)}, u32[]{:S(2)}, u32[]{:S(2)}) collective-permute-start(f32[152,128]{1,0:T(8,128)} %get-tuple-element.21), channel_id=1, source_target_pairs={{0,3},{1,2},{2,1},{3,0},{4,7},{5,6},{6,5},{7,4},{8,11},{9,10},{10,... | collective-permute-start | bytes 233480 | tf_op jit(solution)/shard_map/ppermute | solution.py:542
  21.4 0.0 collective-permute-done.2.refs_1_
  21.4 0.0 copy-start.2
  21.4 2.3 %collective-permute-done.3.refs_2_ = f32[152,128]{1,0:T(8,128)S(1)} collective-permute-done((f32[152,128]{1,0:T(8,128)}, f32[152,128]{1,0:T(8,128)S(1)}, u32[]{:S(2)}, u32[]{:S(2)}) %collective-permute-start.3) | collective-permute-done | bytes 77856 | tf_op jit(solution)/shard_map/ppermute | solution.py:542
  23.7 0.0 copy-start.3
  23.7 2.0 %collective-permute-done.4.refs_3_ = f32[152,128]{1,0:T(8,128)S(1)} collective-permute-done((f32[152,128]{1,0:T(8,128)}, f32[152,128]{1,0:T(8,128)S(1)}, u32[]{:S(2)}, u32[]{:S(2)}) %collective-permute-start.4) | collective-permute-done | bytes 77856 | tf_op jit(solution)/shard_map/ppermute | solution.py:542
  25.7 0.0 copy-start.4
  25.8 0.0 copy-done.2
  25.8 0.0 copy-done.3
  25.8 0.6 %copy-done.4 = f32[152,128]{1,0:T(8,128)} copy-done((f32[152,128]{1,0:T(8,128)}, f32[152,128]{1,0:T(8,128)S(1)}, u32[]{:S(2)}) %copy-start.4) | copy-done | bytes 77848
  26.4 2.3 %collect.1 = f32[3,16,6144]{2,1,0:T(8,128)} custom-call(f32[152,128]{1,0:T(8,128)} %get-tuple-element.18.refs_0_, f32[152,128]{1,0:T(8,128)} %copy-done.2, f32[152,128]{1,0:T(8,128)} %copy-done.3, f32[152,128]{1,0:T(8,128)} %copy-done.4), custom_call_target="tpu_custom_call" | custom-call | tf_op jit(solution)/shard_map/collect/pallas_call | solution.py:543
Async XLA Ops:
  2.5 11.9 %collective-permute-start = (f32[248,128]{1,0:T(8,128)}, f32[248,128]{1,0:T(8,128)S(1)}, u32[]{:S(2)}, u32[]{:S(2)}) collective-permute-start(f32[248,128]{1,0:T(8,128)} %get-tuple-element.12.in_a), channel_id=1, source_target_pairs={{0,4},{4,0},{8,12},{12,8},{16,20},{20,16},{24,28},{28,24},{1,5},{5... | collective-permute-start | bytes 380936 | tf_op jit(solution)/shard_map/ppermute | solution.py:498
  2.8 11.5 %collective-permute-start.1 = (f32[248,128]{1,0:T(8,128)}, f32[248,128]{1,0:T(8,128)S(1)}, u32[]{:S(2)}, u32[]{:S(2)}) collective-permute-start(f32[248,128]{1,0:T(8,128)} %get-tuple-element.13.in_b), channel_id=1, source_target_pairs={{4,8},{8,4},{12,16},{16,12},{20,24},{24,20},{5,9},{9,5},{13,17},{1... | collective-permute-start | bytes 380936 | tf_op jit(solution)/shard_map/ppermute | solution.py:497
  14.4 0.6 %copy-start = (f32[248,128]{1,0:T(8,128)}, f32[248,128]{1,0:T(8,128)S(1)}, u32[]{:S(2)}) copy-start(f32[248,128]{1,0:T(8,128)S(1)} %collective-permute-done.got_a) | copy-start | bytes 380932
  14.4 0.7 %copy-start.1 = (f32[248,128]{1,0:T(8,128)}, f32[248,128]{1,0:T(8,128)S(1)}, u32[]{:S(2)}) copy-start(f32[248,128]{1,0:T(8,128)S(1)} %collective-permute-done.1.got_b) | copy-start | bytes 380932
  18.4 3.0 %collective-permute-start.2 = (f32[152,128]{1,0:T(8,128)}, f32[152,128]{1,0:T(8,128)S(1)}, u32[]{:S(2)}, u32[]{:S(2)}) collective-permute-start(f32[152,128]{1,0:T(8,128)} %get-tuple-element.19), channel_id=1, source_target_pairs={{0,1},{1,0},{2,3},{3,2},{4,5},{5,4},{6,7},{7,6},{8,9},{9,8},{10,11... | collective-permute-start | bytes 233480 | tf_op jit(solution)/shard_map/ppermute | solution.py:542
  19.7 4.0 %collective-permute-start.3 = (f32[152,128]{1,0:T(8,128)}, f32[152,128]{1,0:T(8,128)S(1)}, u32[]{:S(2)}, u32[]{:S(2)}) collective-permute-start(f32[152,128]{1,0:T(8,128)} %get-tuple-element.20), channel_id=1, source_target_pairs={{0,2},{1,3},{2,0},{3,1},{4,6},{5,7},{6,4},{7,5},{8,10},{9,11},{10,... | collective-permute-start | bytes 233480 | tf_op jit(solution)/shard_map/ppermute | solution.py:542
  20.9 4.8 %collective-permute-start.4 = (f32[152,128]{1,0:T(8,128)}, f32[152,128]{1,0:T(8,128)S(1)}, u32[]{:S(2)}, u32[]{:S(2)}) collective-permute-start(f32[152,128]{1,0:T(8,128)} %get-tuple-element.21), channel_id=1, source_target_pairs={{0,3},{1,2},{2,1},{3,0},{4,7},{5,6},{6,5},{7,4},{8,11},{9,10},{10,... | collective-permute-start | bytes 233480 | tf_op jit(solution)/shard_map/ppermute | solution.py:542
  21.4 4.4 %copy-start.2 = (f32[152,128]{1,0:T(8,128)}, f32[152,128]{1,0:T(8,128)S(1)}, u32[]{:S(2)}) copy-start(f32[152,128]{1,0:T(8,128)S(1)} %collective-permute-done.2.refs_1_) | copy-start | bytes 233476
  23.7 2.0 %copy-start.3 = (f32[152,128]{1,0:T(8,128)}, f32[152,128]{1,0:T(8,128)S(1)}, u32[]{:S(2)}) copy-start(f32[152,128]{1,0:T(8,128)S(1)} %collective-permute-done.3.refs_2_) | copy-start | bytes 233476
  25.7 0.6 %copy-start.4 = (f32[152,128]{1,0:T(8,128)}, f32[152,128]{1,0:T(8,128)S(1)}, u32[]{:S(2)}) copy-start(f32[152,128]{1,0:T(8,128)S(1)} %collective-permute-done.4.refs_3_) | copy-start | bytes 233476

commit v2 on v1

--- a/solution.py
+++ b/solution.py
@@ -19,11 +19,13 @@
 OMEGA = 0.8
 
 R_U = 0
-R_V = 96
-R_F = 128
-R_S = 200
-R_G = 224
-PACK = 248
+R_P = 24
+R_S = 96
+R_V = 120
+R_N = 128
+R_E = 136
+R_G = 144
+PACK = 152
 
 T_U = 0
 T_C = 18
@@ -33,7 +35,15 @@
 HALF = PATCH // 2
 ROWS_C = HALF + 2 * (HALF // 4)
 SLOT = 3 * ROWS_C + 8
-UNROLL = 10
+UNROLL = 31
+
+MID = HALF // 4 - 2
+ROW_ORDER = (
+    [0, 1, HALF - 2, HALF - 1, HALF, HALF + MID + 1, HALF + MID + 2, ROWS_C - 1]
+    + list(range(2, HALF - 2))
+    + list(range(HALF + 1, HALF + MID + 1))
+    + list(range(HALF + MID + 3, ROWS_C - 1))
+)
 
 
 def pool_matrix(cz):
@@ -80,11 +90,12 @@
     return up_z(v) - down_z(v)
 
 
-def coefficients(v, v_west, v_east):
+def coefficients(v, v_west, v_east, west=None):
     v_north, v_south = edge_rows(v)
     half = 0.5 * v
     east = half + 0.5 * v_east
-    west = half + 0.5 * v_west
+    if west is None:
+        west = half + 0.5 * v_west
     north = half + 0.5 * v_north
     south = half + 0.5 * v_south
     up = half + 0.5 * up_z(v)
@@ -98,14 +109,18 @@
     )
 
 
+def side_terms(c, u, low, high):
+    y = c[2] * south_of(u, low) + c[3] * north_of(u, high)
+    z = c[4] * down_z(u) + c[5] * up_z(u)
+    return y + z
+
+
 def gather_terms(g, c, u, u_west, u_east, low, high):
     x = c[0] * u_west + c[1] * u_east
-    y = c[2] * south_of(u, low) + c[3] * north_of(u, high)
-    z = c[4] * down_z(u) + c[5] * up_z(u)
-    return (g + x) + (y + z)
-
-
-def pack_kernel(vel, ghost, visc, stress, out_a, out_b, u_s, v_s, s_s, g_s, sem):
+    return (g + x) + side_terms(c, u, low, high)
+
+
+def pack_kernel(vel, ghost, visc, stress, out_a, out_b, own, u_s, v_s, s_s, g_s, sem):
     rows = vel.shape[1]
     copies = []
     for side in range(2):
@@ -125,46 +140,69 @@
     for c in copies:
         c.wait()
     even = lax.axis_index("grp") % 2 == 0
-
-    def plane(ref, side, comp, p):
-        return ref[side, comp, p * CY : (p + 1) * CY, :]
+    xx, yy, zz, xy, xz, yz = range(6)
 
     packs = []
     for side in range(2):
-        parts = {}
-        for c in range(3):
-            parts[R_U + c * 32] = u_s[side, c]
-        parts[R_V] = v_s[side]
-        for j in range(3):
-            p = j if side == 0 else j + 1
-
-            def dx(comp):
-                if p == 0:
-                    return plane(s_s, side, comp, p + 1)
-                if p == 3:
-                    return -plane(s_s, side, comp, p - 1)
-                return plane(s_s, side, comp, p + 1) - plane(s_s, side, comp, p - 1)
-
-            xx, yy, zz, xy, xz, yz = range(6)
-            s_xy, s_xz, s_yz = (plane(s_s, side, k, p) for k in (xy, xz, yz))
-            s_yy, s_zz = (plane(s_s, side, k, p) for k in (yy, zz))
+        sign = -1.0 if side == 0 else 1.0
+
+        def at(d):
+            p = d if side == 0 else 3 - d
+            return slice(p * CY, (p + 1) * CY)
+
+        def dx(comp, d):
+            inner = s_s[side, comp, at(d + 1), :]
+            return -sign * (inner - s_s[side, comp, at(d - 1), :]) if d else -sign * inner
+
+        def ghosts(c, d):
+            r = 2 * (d if side == 0 else 3 - d)
+            return g_s[side, c, r : r + 1, :], g_s[side, c, r + 1 : r + 2, :]
+
+        force = {}
+        for d in range(3):
+            s_xy, s_xz, s_yz, s_yy, s_zz = (s_s[side, k, at(d), :] for k in (xy, xz, yz, yy, zz))
             f = (
-                dx(xx) + diff_y(s_xy) + diff_z(s_xz),
-                dx(xy) + diff_y(s_yy) + diff_z(s_yz),
-                dx(xz) + diff_y(s_yz) + diff_z(s_zz),
+                dx(xx, d) + diff_y(s_xy) + diff_z(s_xz),
+                dx(xy, d) + diff_y(s_yy) + diff_z(s_yz),
+                dx(xz, d) + diff_y(s_yz) + diff_z(s_zz),
             )
             for c in range(3):
-                parts[R_F + (c * 3 + j) * CY] = KAPPA * plane(u_s, side, c, p) + 0.5 * f[c]
-        edge = 0 if side == 0 else 3
+                force[c, d] = KAPPA * u_s[side, c, at(d), :] + 0.5 * f[c]
+        v = [v_s[side, at(d), :] for d in range(4)]
+        coef, scale = {}, {}
+        for d in (1, 2):
+            coef[d], _, scale[d] = coefficients(v[d], v[d - 1], v[d + 1])
+        face = 0.5 * v[0] + 0.5 * v[1]
+        parts = {R_V: v[0], R_N: face, R_E: face * coef[1][0]}
         for c, k in enumerate((xx, xy, xz)):
-            parts[R_S + c * CY] = plane(s_s, side, k, edge)
-        for c in range(3):
-            parts[R_G + c * 8] = g_s[side, c]
+            u = [u_s[side, c, at(d), :] for d in range(4)]
+            once = {}
+            for d in (1, 2):
+                low, high = ghosts(c, d)
+                t = gather_terms(
+                    scale[d] * force[c, d], coef[d], u[d], u[d - 1], u[d + 1], low, high
+                )
+                once[d] = (1.0 - OMEGA) * u[d] + t
+            low, high = ghosts(c, 1)
+            rest = side_terms(coef[1], once[1], low, high)
+            twice = (1.0 - OMEGA) * once[1] + (
+                scale[1] * force[c, 1] + coef[1][1] * once[2] + rest
+            )
+            for n, inner in enumerate((u[1], once[1], twice)):
+                parts[R_P + (n * 3 + c) * CY] = force[c, 0] + face * inner
+            parts[R_U + c * CY] = u[0]
+            parts[R_S + c * CY] = s_s[side, k, at(0), :]
+            own[side, c * CY : (c + 1) * CY, :] = force[c, 0]
+            own[side, (3 + c) * CY : (4 + c) * CY, :] = s_s[side, k, at(0), :]
+            low, high = ghosts(c, 0)
+            parts[R_G + 2 * c], parts[R_G + 2 * c + 1] = low, high
         packs.append(parts)
     for r, low in packs[0].items():
         high = packs[1][r]
         out_a[r : r + low.shape[0], :] = jnp.where(even, high, low)
         out_b[r : r + low.shape[0], :] = jnp.where(even, low, high)
+    for out in (out_a, out_b):
+        out[R_G + 6 :, :] = jnp.zeros_like(out[R_G + 6 :, :])
 
 
 def split_dot(x, m):
@@ -190,8 +228,26 @@
 
 
 def interior_kernel(
-    vel, ghost, visc, stress, pool, new_v, state, pooled, coef, gsrc, ua, ub, s_sum, flux, xmat
+    vel,
+    ghost,
+    visc,
+    stress,
+    pool_hbm,
+    new_v,
+    state,
+    pooled,
+    pool,
+    coef,
+    gsrc,
+    ua,
+    ub,
+    s_sum,
+    flux,
+    xmat,
+    sem,
 ):
+    pool_copy = pltpu.make_async_copy(pool_hbm, pool, sem)
+    pool_copy.start()
     planes = visc.shape[0] // CY
     cz = visc.shape[1]
 
@@ -275,13 +331,20 @@
                 both = flux[pl.ds(2 * j, planes // 8, stride=8), :] + flux[
                     pl.ds(2 * j + 1, planes // 8, stride=8), :
                 ]
-                base = k * ROWS_C + HALF + face * (HALF // 4)
-                xmat[base : base + HALF // 4, j * cz : (j + 1) * cz] = 0.25 * both
+                cols = slice(j * cz, (j + 1) * cz)
+                both = 0.25 * both
+                first, last = k * ROWS_C + 4 + 2 * face, k * ROWS_C + HALF + 4 + face * MID
+                xmat[first : first + 1, cols] = both[:1]
+                xmat[first + 1 : first + 2, cols] = both[MID + 1 :]
+                xmat[last : last + MID, cols] = both[1 : MID + 1]
         for j in range(4):
             both = s_sum[k, pl.ds(2 * j, planes // 2, stride=CY), :] + s_sum[
                 k, pl.ds(2 * j + 1, planes // 2, stride=CY), :
             ]
-            xmat[k * ROWS_C : k * ROWS_C + HALF, j * cz : (j + 1) * cz] = 0.125 * both
+            cols = slice(j * cz, (j + 1) * cz)
+            xmat[k * ROWS_C : k * ROWS_C + 4, cols] = jnp.zeros((4, cz), jnp.float32)
+            xmat[k * ROWS_C + 8 : k * ROWS_C + HALF + 4, cols] = 0.125 * both[2 : HALF - 2]
+    pool_copy.wait()
     pooled[...] = split_dot(xmat[...], pool[...])
 
     for side in range(2):
@@ -308,10 +371,12 @@
     n_wide,
     owner,
     mask,
-    in_a,
-    in_b,
+    own,
     got_a,
     got_b,
+    vel,
+    ghost,
+    visc,
     state,
     pooled,
     pool,
@@ -320,93 +385,119 @@
     *refs,
 ):
     slots = refs[:n_wide]
-    u_out, xmat, flux, total_s, out_sem = refs[n_wide:]
-    del velocity_in
+    u_out, xmat, flux, out_sem = refs[n_wide:]
+    rows = velocity_out.shape[1]
+    inner = pl.ds(SWEEPS * CY, rows - 2 * SWEEPS * CY)
+    inner_copy = pltpu.make_async_copy(
+        velocity_in.at[:, inner], velocity_out.at[:, inner], out_sem.at[2]
+    )
+    inner_copy.start()
     grp = lax.axis_index("grp")
     even = grp % 2 == 0
     ends = (grp > 0, grp < lax.axis_size("grp") - 1)
-
     cz = pool.shape[0] // 4
+
+    me = lax.axis_index("wide")
+    weights = []
+    for d in range(n_wide):
+        local, weight = jnp.float32(-1.0), []
+        for p in range(P_SIZE):
+            match = owner[0, p] // CP_DEV == me ^ d
+            weight.append(jnp.where(match, mask[0, p], 0).astype(jnp.float32))
+            local = jnp.where(match, (owner[0, p] % CP_DEV).astype(jnp.float32), local)
+        weights.append(weight)
+        slots[d][3 * ROWS_C :, :] = jnp.full((8, cz), local, jnp.float32)
+
+    def weighted(d, value):
+        total = None
+        for p in range(P_SIZE):
+            term = value[:, p * cz : (p + 1) * cz] * weights[d][p]
+            total = term if total is None else total + term
+        return total
+
+    for k in range(3):
+        part = slice(k * ROWS_C + 8, (k + 1) * ROWS_C)
+        value = pooled[part, :]
+        for d in range(n_wide):
+            slots[d][part, :] = weighted(d, value)
+
     xmat[...] = jnp.zeros_like(xmat)
     flux[...] = jnp.zeros_like(flux)
     for side in range(2):
         sign = -1.0 if side == 0 else 1.0
         inside = jnp.where(ends[side], 1.0, 0.0)
 
-        def index(q, count):
-            if q >= 0:
-                return q if side == 0 else count - 1 - q
-            return count + q if side == 0 else -q - 1
-
-        def get(q, start, comp, count, rows=CY):
-            r = start + (comp * count + index(q, count)) * rows
-            return packed(q >= 0, r, rows)
-
-        def packed(own, r, rows=CY):
-            a, b = (in_a, in_b) if own else (got_a, got_b)
-            a, b = a[r : r + rows, :], b[r : r + rows, :]
+        def at(d):
+            i = d if side == 0 else rows // CY - 1 - d
+            return slice(i * CY, (i + 1) * CY)
+
+        def halo(r, count=CY):
+            a, b = got_a[r : r + count, :], got_b[r : r + count, :]
             return jnp.where(even, b, a) if side == 0 else jnp.where(even, a, b)
+
+        def ghosts(k, d):
+            if d < 0:
+                return halo(R_G + 2 * k, 1), halo(R_G + 2 * k + 1, 1)
+            r = 2 * (d if side == 0 else rows // CY - 1 - d)
+            return ghost[k, r : r + 1, :], ghost[k, r + 1 : r + 2, :]
 
         def saved(n):
             return state[side, n * CY : (n + 1) * CY, :]
 
-        visc = {q: get(q, R_V, 0, 4) for q in range(-4, 2)}
-        ghost = {
-            (k, q): get(q, R_G, k, 4, 2) for k in range(3) for q in range(-3, 4)
-        }
-        coef, diag, g = {}, {}, {}
-        for q in range(-3, 1):
-            c, d, scale = coefficients(visc[q], visc[q - 1], visc[q + 1])
-            coef[q], diag[q] = c, d
-            for k in range(3):
-                f = get(q, R_F, k, 3)
-                if q == 0:
-                    f = f + (0.5 * sign) * packed(False, R_S + k * CY)
-                if q == -1:
-                    f = f - (0.5 * sign) * packed(True, R_S + k * CY)
-                g[k, q] = scale * f
-        for q in range(1, 4):
-            c = [saved(T_C + n * 3 + q - 1) for n in range(7)]
-            coef[q], diag[q] = ([c[0], c[1]] if side == 0 else [c[1], c[0]]) + c[2:6], c[6]
-            for k in range(3):
-                g[k, q] = saved(T_G + k * 3 + q - 1)
+        v_halo, v_own = halo(R_V), visc[at(0), :]
+        coef, diag = {}, {}
+        coef[-1], _, halo_scale = coefficients(v_halo, None, v_own, halo(R_N))
+        coef[0], diag[0], own_scale = coefficients(v_own, v_halo, visc[at(1), :])
+        for d in range(1, 4):
+            c = [saved(T_C + n * 3 + d - 1) for n in range(7)]
+            coef[d], diag[d] = ([c[0], c[1]] if side == 0 else [c[1], c[0]]) + c[2:6], c[6]
         for k in range(3):
-            u = {q: get(q, R_U, k, 4) for q in range(-4, 2)}
+            part = slice(k * CY, (k + 1) * CY)
+            own_stress = own[side, (3 + k) * CY : (4 + k) * CY, :]
+            g = {0: own_scale * (own[side, part, :] + (0.5 * sign) * halo(R_S + k * CY))}
+            for d in range(1, 4):
+                g[d] = saved(T_G + k * 3 + d - 1)
+            low, high = ghosts(k, -1)
+            u = {-1: halo(R_U + k * CY), 0: vel[k, at(0), :], 1: vel[k, at(1), :]}
             for s in range(1, SWEEPS + 1):
-                new = {}
-                for q in range(s - 4, s):
-                    low, high = ghost[k, q][0:1], ghost[k, q][1:2]
-                    t = gather_terms(g[k, q], coef[q], u[q], u[q - 1], u[q + 1], low, high)
-                    value = (1.0 - OMEGA) * u[q] + t
-                    new[q] = value * inside if q < 0 else value
+                known = halo(R_P + ((s - 1) * 3 + k) * CY) - (0.5 * sign) * own_stress
+                if s == 1:
+                    first = None
+                elif s == 2:
+                    first = u[-1]
+                else:
+                    known = known + halo(R_E) * first
+                t = halo_scale * known + (
+                    coef[-1][1] * u[0] + side_terms(coef[-1], u[-1], low, high)
+                )
+                new = {-1: ((1.0 - OMEGA) * u[-1] + t) * inside}
+                for d in range(s):
+                    t = gather_terms(g[d], coef[d], u[d], u[d - 1], u[d + 1], *ghosts(k, d))
+                    new[d] = (1.0 - OMEGA) * u[d] + t
                 for e in range(2):
                     new[s + e] = saved(T_U + (s - 1) * 6 + k * 2 + e)
                 u = new
-            for q in range(3):
-                i = q if side == 0 else 2 - q
-                u_out[side, k, i * CY : (i + 1) * CY, :] = u[q]
-            sums = []
+            for d in range(SWEEPS):
+                i = d if side == 0 else SWEEPS - 1 - d
+                u_out[side, k, i * CY : (i + 1) * CY, :] = u[d]
             for b in range(2):
                 total = None
-                for q in (2 * b, 2 * b + 1):
-                    low, high = ghost[k, q][0:1], ghost[k, q][1:2]
-                    t = gather_terms(g[k, q], coef[q], u[q], u[q - 1], u[q + 1], low, high)
-                    r = (t - OMEGA * u[q]) * diag[q]
+                for d in (2 * b, 2 * b + 1):
+                    t = gather_terms(g[d], coef[d], u[d], u[d - 1], u[d + 1], *ghosts(k, d))
+                    r = (t - OMEGA * u[d]) * diag[d]
                     total = r if total is None else total + r
-                sums.append(total)
-            for b in range(2):
                 row = b if side == 0 else 3 - b
-                both = sums[b] + pltpu.roll(sums[b], CY - 1, 0)
+                both = total + pltpu.roll(total, CY - 1, 0)
                 for j in range(4):
                     xmat[k * 8 + row : k * 8 + row + 1, j * cz : (j + 1) * cz] = (
                         0.125 * both[2 * j : 2 * j + 1, :]
                     )
-            for q in range(3):
-                x = q if side == 0 else 7 - q
-                nu = get(q, R_V, 0, 4)
-                low, high = ghost[k, q][0:1], ghost[k, q][1:2]
-                flux[side, k, 0, x : x + 1, :] = nu[0:1] * (u[q][0:1] - low)
-                flux[side, k, 1, x : x + 1, :] = nu[CY - 1 :] * (high - u[q][CY - 1 :])
+            for d in range(SWEEPS):
+                x = d if side == 0 else 7 - d
+                nu = visc[at(d), :]
+                low, high = ghosts(k, d)
+                flux[side, k, 0, x : x + 1, :] = nu[0:1] * (u[d][0:1] - low)
+                flux[side, k, 1, x : x + 1, :] = nu[CY - 1 :] * (high - u[d][CY - 1 :])
             for face in range(2):
                 for j in range(4):
                     row = k * 8 + 4 + face * 2 + side
@@ -414,11 +505,10 @@
                         flux[side, k, face, 2 * j : 2 * j + 1, :]
                         + flux[side, k, face, 2 * j + 1 : 2 * j + 2, :]
                     )
-    rows = velocity_out.shape[1]
     out_copies = [
         pltpu.make_async_copy(
             u_out.at[side],
-            velocity_out.at[:, pl.ds(0 if side == 0 else rows - 3 * CY, 3 * CY)],
+            velocity_out.at[:, pl.ds(0 if side == 0 else rows - SWEEPS * CY, SWEEPS * CY)],
             out_sem.at[side],
         )
         for side in range(2)
@@ -427,25 +517,14 @@
         c.start()
 
     edge = split_dot(xmat[...], pool[...])
-    places = (0, 1, HALF - 2, HALF - 1, HALF, HALF + HALF // 4 - 1, HALF + HALF // 4, ROWS_C - 1)
-    total_s[...] = pooled[...]
     for k in range(3):
-        for n, place in enumerate(places):
-            r = k * ROWS_C + place
-            total_s[r : r + 1, :] = total_s[r : r + 1, :] + edge[k * 8 + n : k * 8 + n + 1, :]
-    me = lax.axis_index("wide")
-    for d in range(n_wide):
-        value, local = None, jnp.float32(-1.0)
-        for p in range(P_SIZE):
-            match = owner[0, p] // CP_DEV == me ^ d
-            weight = jnp.where(match, mask[0, p], 0).astype(jnp.float32)
-            local = jnp.where(match, (owner[0, p] % CP_DEV).astype(jnp.float32), local)
-            term = total_s[:, p * cz : (p + 1) * cz] * weight
-            value = term if value is None else value + term
-        slots[d][0 : 3 * ROWS_C, :] = value
-        slots[d][3 * ROWS_C :, :] = jnp.full((8, cz), local, jnp.float32)
+        part = slice(k * ROWS_C, k * ROWS_C + 8)
+        value = pooled[part, :] + edge[k * 8 : (k + 1) * 8]
+        for d in range(n_wide):
+            slots[d][part, :] = weighted(d, value)
     for c in out_copies:
         c.wait()
+    inner_copy.wait()
 
 
 def collect_kernel(n_wide, *refs):
@@ -454,10 +533,10 @@
     rows = lax.broadcasted_iota(jnp.int32, (CP_DEV, cz), 0).astype(jnp.float32)
     takes = [rows == slot[3 * ROWS_C : 3 * ROWS_C + 1, :] for slot in slots]
     for k in range(3):
-        for n in range(ROWS_C):
+        for place, n in enumerate(ROW_ORDER):
             total = None
             for take, slot in zip(takes, slots, strict=True):
-                r = k * ROWS_C + n
+                r = k * ROWS_C + place
                 term = jnp.where(take, slot[r : r + 1, :], 0.0)
                 total = term if total is None else total + term
             out[k, :, n * cz : (n + 1) * cz] = total
@@ -473,15 +552,15 @@
     strs = stress.reshape(6, cells_x * CY, cz)
     pool = jnp.asarray(pool_matrix(cz), jnp.bfloat16)
 
-    anywhere = pl.BlockSpec(memory_space=pl.ANY)
+    anywhere = pl.BlockSpec(memory_space=pltpu.HBM)
     vmem = pl.BlockSpec(memory_space=pltpu.VMEM)
     smem = pl.BlockSpec(memory_space=pltpu.SMEM)
     pack_shape = jax.ShapeDtypeStruct((PACK, cz), f32)
-    pack_a, pack_b = pl.pallas_call(
+    pack_a, pack_b, own = pl.pallas_call(
         pack_kernel,
-        out_shape=(pack_shape, pack_shape),
+        out_shape=(pack_shape, pack_shape, jax.ShapeDtypeStruct((2, 6 * CY, cz), f32)),
         in_specs=[anywhere] * 4,
-        out_specs=(vmem, vmem),
+        out_specs=(vmem, vmem, vmem),
         scratch_shapes=[
             pltpu.VMEM((2, 3, 4 * CY, cz), f32),
             pltpu.VMEM((2, 4 * CY, cz), f32),
@@ -489,8 +568,9 @@
             pltpu.VMEM((2, 3, 8, cz), f32),
             pltpu.SemaphoreType.DMA((2, 4)),
         ],
+        compiler_params=pltpu.CompilerParams(vmem_limit_bytes=4 * 2**20),
         name="pack",
-    )(vel, ghost, visc, strs)
+    )(*(pltpu.with_memory_space_constraint(x, pltpu.HBM) for x in (vel, ghost, visc, strs)))
 
     pairs_a = [(i, i ^ 1) for i in range(n_grp) if i ^ 1 < n_grp]
     pairs_b = [(i, j) for i in range(n_grp) for j in [((i + 1) ^ 1) - 1] if 0 <= j < n_grp]
@@ -498,15 +578,16 @@
     got_a = lax.ppermute(pack_a, "grp", pairs_a)
 
     rows = cells_x * CY
-    new_v, state, pooled = pl.pallas_call(
+    new_v, state, pooled, pool = pl.pallas_call(
         interior_kernel,
         out_shape=(
             jax.ShapeDtypeStruct((3, rows, cz), f32),
             jax.ShapeDtypeStruct((2, STATE * CY, cz), f32),
             jax.ShapeDtypeStruct((3 * ROWS_C, P_SIZE * cz), f32),
+            jax.ShapeDtypeStruct(pool.shape, pool.dtype),
         ),
-        in_specs=[vmem] * 5,
-        out_specs=(vmem, vmem, vmem),
+        in_specs=[vmem] * 4 + [anywhere],
+        out_specs=(vmem, vmem, vmem, vmem),
         scratch_shapes=[
             pltpu.VMEM((7, rows, cz), f32),
             pltpu.VMEM((3, rows, cz), f32),
@@ -515,27 +596,28 @@
             pltpu.VMEM((3, rows // 2, cz), f32),
             pltpu.VMEM((cells_x, cz), f32),
             pltpu.VMEM((3 * ROWS_C, 4 * cz), f32),
+            pltpu.SemaphoreType.DMA,
         ],
         cost_estimate=pl.CostEstimate(flops=100_000_000, bytes_accessed=4_000_000, transcendentals=0),
+        compiler_params=pltpu.CompilerParams(vmem_limit_bytes=20 * 2**20),
         name="interior",
-    )(vel, ghost, visc, strs, pool)
+    )(vel, ghost, visc, strs, pltpu.with_memory_space_constraint(pool, pltpu.HBM))
 
     slot_shape = jax.ShapeDtypeStruct((SLOT, cz), f32)
     outs = pl.pallas_call(
         functools.partial(edge_kernel, n_wide),
         out_shape=(jax.ShapeDtypeStruct(new_v.shape, f32),) + (slot_shape,) * n_wide,
-        in_specs=[smem, smem] + [vmem] * 7 + [anywhere],
+        in_specs=[smem, smem] + [vmem] * 10,
         out_specs=(anywhere,) + (vmem,) * n_wide,
         scratch_shapes=[
             pltpu.VMEM((2, 3, 3 * CY, cz), f32),
             pltpu.VMEM((24, 4 * cz), f32),
             pltpu.VMEM((2, 3, 2, 8, cz), f32),
-            pltpu.VMEM((3 * ROWS_C, P_SIZE * cz), f32),
-            pltpu.SemaphoreType.DMA((2,)),
+            pltpu.SemaphoreType.DMA((3,)),
         ],
-        input_output_aliases={9: 0},
+        compiler_params=pltpu.CompilerParams(vmem_limit_bytes=8 * 2**20),
         name="edge",
-    )(coarse_owner, patch_mask, pack_a, pack_b, got_a, got_b, state, pooled, pool, new_v)
+    )(coarse_owner, patch_mask, own, got_a, got_b, vel, ghost, visc, state, pooled, pool, new_v)
     smoothed, slots = outs[0], list(outs[1:])
 
     for k in range(1, n_wide):
@@ -545,6 +627,7 @@
         out_shape=jax.ShapeDtypeStruct((3, CP_DEV, PV), f32),
         in_specs=[vmem] * n_wide,
         out_specs=vmem,
+        compiler_params=pltpu.CompilerParams(vmem_limit_bytes=8 * 2**20),
         name="collect",
     )(*slots)
     return smoothed.reshape(velocity.shape), coarse.transpose(1, 0, 2)[None]

time: 28.9 us -> 20.9 us (0.72)
  Pallas kernels: 14.9 us -> 8.22 us
  local copies, waits for them, and re-layouts: 1.3 us -> 0.03 us
    pallas_call x1, Pallas kernels: 7.4 us -> 3.54 us  [on_device(): pl.pallas_call(interior_kernel, out_shape=(jax.ShapeDtypeStruct((3, rows,...]
    pallas_call x1, Pallas kernels: 3.3 us -> 1.93 us  [on_device(): pl.pallas_call(functools.partial(edge_kernel, n_wide), out_shape=(jax.Sha...]
    unnamed x10 -> x12, local copies, waits for them, and re-layouts: 1.3 us -> 0.03 us
    pallas_call x1, Pallas kernels: 2.28 us -> 1.28 us  [on_device(): pl.pallas_call(functools.partial(collect_kernel, n_wide), out_shape=jax.S...]
    pallas_call x1, Pallas kernels: 1.89 us -> 1.47 us  [on_device(): pl.pallas_call(pack_kernel, out_shape=(pack_shape, pack_shape, jax.ShapeD...]
  transfers between devices with their start and end apart: 5 -> 5, of which waited for: 2 -> 2; matrix products, arithmetic and copies ran while one was open for 0% -> 0% of each run, Pallas kernels for 26% -> 17%
where the time goes in v2:
time: 20.9 us; the launch traced here: 20.6 us
  Pallas kernels  8.22 us (39%)
  starting transfers between devices  7.45 us (36%)
  waiting for transfers between devices  4.15 us (20%)
  between operations  0.78 us (4%)
    ppermute x3, waiting for transfers between devices, on_device(): lax.ppermute(slots[k], 'wide', [(i, i ^ k) for i in range(n_wide)])  4.15 us
    ppermute x1, starting transfers between devices, on_device(): got_b = lax.ppermute(pack_b, 'grp', pairs_b)  4.12 us
    pallas_call x1, Pallas kernels, on_device(): pl.pallas_call(interior_kernel, out_shape=(jax.ShapeDtypeStruct((3, rows,...  3.54 us
    ppermute x3, starting transfers between devices, on_device(): lax.ppermute(slots[k], 'wide', [(i, i ^ k) for i in range(n_wide)])  3.01 us
    pallas_call x1, Pallas kernels, on_device(): pl.pallas_call(functools.partial(edge_kernel, n_wide), out_shape=(jax.Sha...  1.93 us
    pallas_call x1, Pallas kernels, on_device(): pl.pallas_call(pack_kernel, out_shape=(pack_shape, pack_shape, jax.ShapeD...  1.47 us
    pallas_call x1, Pallas kernels, on_device(): pl.pallas_call(functools.partial(collect_kernel, n_wide), out_shape=jax.S...  1.28 us
  transfers between devices with their start and end apart: 5, of which 2 were waited for; matrix products, arithmetic and copies ran while one was open for 0% of the time, Pallas kernels for 17%

profile of v2, /device:TPU:11, one launch (start us, length us, event | category | flops | bytes accessed | tf_op | source)
XLA Modules:
  0.0 20.6 jit_solution(5553569899053661091)
XLA Ops:
  0.6 0.0 copy-start.1
  0.6 0.0 copy-start.2
  0.7 0.0 copy-start.3
  0.7 0.0 copy-start
  0.7 1.5 %pack.1 = (f32[152,128]{1,0:T(8,128)S(1)}, f32[152,128]{1,0:T(8,128)S(1)}, f32[2,48,128]{2,1,0:T(8,128)S(1)}) custom-call(f32[3,512,128]{2,1,0:T(8,128)} %bitcast.8, f32[3,128,128]{2,1,0:T(8,128)} %bitcast.16, f32[512,128]{1,0:T(8,128)} %bitcast.13, f32[6,512,128]{2,1,0:T(8,128)} %bitcast.11), custom_call_target="tpu_custom_call" | custom-call | tf_op jit(solution)/shard_map/pack/pallas_call | solution.py:559
  2.1 0.0 copy-start.4
  2.2 0.0 copy-start.5
  2.2 0.3 %collective-permute-start = (f32[152,128]{1,0:T(8,128)S(1)}, f32[152,128]{1,0:T(8,128)S(1)}, u32[]{:S(2)}, u32[]{:S(2)}) collective-permute-start(f32[152,128]{1,0:T(8,128)S(1)} %get-tuple-element.15), channel_id=1, source_target_pairs={{0,4},{4,0},{8,12},{12,8},{16,20},{20,16},{24,28},{28,24},{1,5},{5... | collective-permute-start | bytes 233480 | tf_op jit(solution)/shard_map/ppermute | solution.py:578
  2.5 4.1 %collective-permute-start.1 = (f32[152,128]{1,0:T(8,128)S(1)}, f32[152,128]{1,0:T(8,128)S(1)}, u32[]{:S(2)}, u32[]{:S(2)}) collective-permute-start(f32[152,128]{1,0:T(8,128)S(1)} %get-tuple-element.16), channel_id=1, source_target_pairs={{4,8},{8,4},{12,16},{16,12},{20,24},{24,20},{5,9},{9,5},{13,17},{1... | collective-permute-start | bytes 233480 | tf_op jit(solution)/shard_map/ppermute | solution.py:577
  6.6 0.0 copy-done.1
  6.6 0.0 copy-done.2
  6.6 0.0 copy-done.3
  6.7 0.0 copy-done
  6.7 3.5 %interior.1 = (f32[3,512,128]{2,1,0:T(8,128)S(1)}, f32[2,384,128]{2,1,0:T(8,128)S(1)}, f32[144,256]{1,0:T(8,128)S(1)}, bf16[512,256]{1,0:T(8,128)(2,1)S(1)}) custom-call(f32[3,512,128]{2,1,0:T(8,128)S(1)} %bitcast.9, f32[3,128,128]{2,1,0:T(8,128)S(1)} %bitcast.17, f32[512,128]{1,0:T(8,128)S(1)} %bitcast.14, f32[6,512,128]{2,1,0:T(8,128)S(1)} %bitcast.12, ...), custom_call_target="tpu_custom_call" | custom-call | flops 100000000 | bytes 4000000 | tf_op jit(solution)/shard_map/interior/pallas_call | solution.py:581
  10.2 0.0 collective-permute-done.got_a
  10.2 0.0 collective-permute-done.1.got_b
  10.2 0.0 copy-done.4
  10.2 0.0 copy-done.5
  10.2 1.9 %edge.1 = (f32[3,512,128]{2,1,0:T(8,128)}, f32[152,128]{1,0:T(8,128)S(1)}, f32[152,128]{1,0:T(8,128)S(1)}, f32[152,128]{1,0:T(8,128)S(1)}, f32[152,128]{1,0:T(8,128)S(1)}) custom-call(s32[1,2]{1,0:T(1,128)S(1)} %copy-done.4, s32[1,2]{1,0:T(1,128)S(1)} %copy-done.5, f32[2,48,128]{2,1,0:T(8,128)S(1)} %get-tuple-element.14.own, ...), custom_call_target="tpu_custom_call" | custom-call | tf_op jit(solution)/shard_map/edge/pallas_call | solution.py:607
  12.2 1.3 %collective-permute-start.2 = (f32[152,128]{1,0:T(8,128)S(1)}, f32[152,128]{1,0:T(8,128)S(1)}, u32[]{:S(2)}, u32[]{:S(2)}) collective-permute-start(f32[152,128]{1,0:T(8,128)S(1)} %get-tuple-element.23), channel_id=1, source_target_pairs={{0,1},{1,0},{2,3},{3,2},{4,5},{5,4},{6,7},{7,6},{8,9},{9,8},{10,11... | collective-permute-start | bytes 233480 | tf_op jit(solution)/shard_map/ppermute | solution.py:624
  13.5 1.2 %collective-permute-start.3 = (f32[152,128]{1,0:T(8,128)S(1)}, f32[152,128]{1,0:T(8,128)S(1)}, u32[]{:S(2)}, u32[]{:S(2)}) collective-permute-start(f32[152,128]{1,0:T(8,128)S(1)} %get-tuple-element.24), channel_id=1, source_target_pairs={{0,2},{1,3},{2,0},{3,1},{4,6},{5,7},{6,4},{7,5},{8,10},{9,11},{10,... | collective-permute-start | bytes 233480 | tf_op jit(solution)/shard_map/ppermute | solution.py:624
  14.7 0.5 %collective-permute-start.4 = (f32[152,128]{1,0:T(8,128)S(1)}, f32[152,128]{1,0:T(8,128)S(1)}, u32[]{:S(2)}, u32[]{:S(2)}) collective-permute-start(f32[152,128]{1,0:T(8,128)S(1)} %get-tuple-element.25), channel_id=1, source_target_pairs={{0,3},{1,2},{2,1},{3,0},{4,7},{5,6},{6,5},{7,4},{8,11},{9,10},{10,... | collective-permute-start | bytes 233480 | tf_op jit(solution)/shard_map/ppermute | solution.py:624
  15.2 0.0 collective-permute-done.2.refs_1_
  15.2 2.1 %collective-permute-done.3.refs_2_ = f32[152,128]{1,0:T(8,128)S(1)} collective-permute-done((f32[152,128]{1,0:T(8,128)S(1)}, f32[152,128]{1,0:T(8,128)S(1)}, u32[]{:S(2)}, u32[]{:S(2)}) %collective-permute-start.3) | collective-permute-done | bytes 77856 | tf_op jit(solution)/shard_map/ppermute | solution.py:624
  17.3 2.0 %collective-permute-done.4.refs_3_ = f32[152,128]{1,0:T(8,128)S(1)} collective-permute-done((f32[152,128]{1,0:T(8,128)S(1)}, f32[152,128]{1,0:T(8,128)S(1)}, u32[]{:S(2)}, u32[]{:S(2)}) %collective-permute-start.4) | collective-permute-done | bytes 77856 | tf_op jit(solution)/shard_map/ppermute | solution.py:624
  19.3 1.3 %collect.1 = f32[3,16,6144]{2,1,0:T(8,128)} custom-call(f32[152,128]{1,0:T(8,128)S(1)} %get-tuple-element.22.refs_0_, f32[152,128]{1,0:T(8,128)S(1)} %collective-permute-done.2.refs_1_, f32[152,128]{1,0:T(8,128)S(1)} %collective-permute-done.3.refs_2_, f32[152,128]{1,0:T(8,128)S(1)} %collective-permute-done.4.refs_3_), custom_call_target="tpu_custom_call" | custom-call | tf_op jit(solution)/shard_map/collect/pallas_call | solution.py:625
Async XLA Ops:
  0.6 6.0 %copy-start.1 = (f32[6,64,8,128]{3,2,1,0:T(8,128)S(1)}, f32[6,64,8,128]{3,2,1,0:T(8,128)}, u32[]{:S(2)}) copy-start(f32[6,64,8,128]{3,2,1,0:T(8,128)} %param.10) | copy-start | bytes 4718596
  0.6 6.0 %copy-start.2 = (f32[64,8,128]{2,1,0:T(8,128)S(1)}, f32[64,8,128]{2,1,0:T(8,128)}, u32[]{:S(2)}) copy-start(f32[64,8,128]{2,1,0:T(8,128)} %param.9) | copy-start | bytes 786436
  0.7 6.0 %copy-start.3 = (f32[3,64,2,128]{3,2,1,0:T(2,128)S(1)}, f32[3,64,2,128]{3,2,1,0:T(2,128)}, u32[]{:S(2)}) copy-start(f32[3,64,2,128]{3,2,1,0:T(2,128)} %param.8) | copy-start | bytes 589828
  0.7 6.0 %copy-start = (f32[3,64,8,128]{3,2,1,0:T(8,128)S(1)}, f32[3,64,8,128]{3,2,1,0:T(8,128)}, u32[]{:S(2)}) copy-start(f32[3,64,8,128]{3,2,1,0:T(8,128)} %param.7) | copy-start | bytes 2359300
  2.1 8.1 %copy-start.4 = (s32[1,2]{1,0:T(1,128)S(1)}, s32[1,2]{1,0:T(1,128)}, u32[]{:S(2)}) copy-start(s32[1,2]{1,0:T(1,128)} %owner.1) | copy-start | bytes 28
  2.2 8.1 %copy-start.5 = (s32[1,2]{1,0:T(1,128)S(1)}, s32[1,2]{1,0:T(1,128)}, u32[]{:S(2)}) copy-start(s32[1,2]{1,0:T(1,128)} %mask.1) | copy-start | bytes 28
  2.2 8.0 %collective-permute-start = (f32[152,128]{1,0:T(8,128)S(1)}, f32[152,128]{1,0:T(8,128)S(1)}, u32[]{:S(2)}, u32[]{:S(2)}) collective-permute-start(f32[152,128]{1,0:T(8,128)S(1)} %get-tuple-element.15), channel_id=1, source_target_pairs={{0,4},{4,0},{8,12},{12,8},{16,20},{20,16},{24,28},{28,24},{1,5},{5... | collective-permute-start | bytes 233480 | tf_op jit(solution)/shard_map/ppermute | solution.py:578
  2.5 7.7 %collective-permute-start.1 = (f32[152,128]{1,0:T(8,128)S(1)}, f32[152,128]{1,0:T(8,128)S(1)}, u32[]{:S(2)}, u32[]{:S(2)}) collective-permute-start(f32[152,128]{1,0:T(8,128)S(1)} %get-tuple-element.16), channel_id=1, source_target_pairs={{4,8},{8,4},{12,16},{16,12},{20,24},{24,20},{5,9},{9,5},{13,17},{1... | collective-permute-start | bytes 233480 | tf_op jit(solution)/shard_map/ppermute | solution.py:577
  12.2 3.0 %collective-permute-start.2 = (f32[152,128]{1,0:T(8,128)S(1)}, f32[152,128]{1,0:T(8,128)S(1)}, u32[]{:S(2)}, u32[]{:S(2)}) collective-permute-start(f32[152,128]{1,0:T(8,128)S(1)} %get-tuple-element.23), channel_id=1, source_target_pairs={{0,1},{1,0},{2,3},{3,2},{4,5},{5,4},{6,7},{7,6},{8,9},{9,8},{10,11... | collective-permute-start | bytes 233480 | tf_op jit(solution)/shard_map/ppermute | solution.py:624
  13.5 3.8 %collective-permute-start.3 = (f32[152,128]{1,0:T(8,128)S(1)}, f32[152,128]{1,0:T(8,128)S(1)}, u32[]{:S(2)}, u32[]{:S(2)}) collective-permute-start(f32[152,128]{1,0:T(8,128)S(1)} %get-tuple-element.24), channel_id=1, source_target_pairs={{0,2},{1,3},{2,0},{3,1},{4,6},{5,7},{6,4},{7,5},{8,10},{9,11},{10,... | collective-permute-start | bytes 233480 | tf_op jit(solution)/shard_map/ppermute | solution.py:624
  14.7 4.6 %collective-permute-start.4 = (f32[152,128]{1,0:T(8,128)S(1)}, f32[152,128]{1,0:T(8,128)S(1)}, u32[]{:S(2)}, u32[]{:S(2)}) collective-permute-start(f32[152,128]{1,0:T(8,128)S(1)} %get-tuple-element.25), channel_id=1, source_target_pairs={{0,3},{1,2},{2,1},{3,0},{4,7},{5,6},{6,5},{7,4},{8,11},{9,10},{10,... | collective-permute-start | bytes 233480 | tf_op jit(solution)/shard_map/ppermute | solution.py:624

commit v3 on v2

--- a/solution.py
+++ b/solution.py
@@ -7,6 +7,7 @@
 from jax.experimental import pallas as pl
 from jax.experimental.pallas import tpu as pltpu
 from jax.sharding import PartitionSpec as P
+
 
 PATCH = 64
 CY = 8
@@ -36,6 +37,7 @@
 ROWS_C = HALF + 2 * (HALF // 4)
 SLOT = 3 * ROWS_C + 8
 UNROLL = 31
+PIECES = 2
 
 MID = HALF // 4 - 2
 ROW_ORDER = (
@@ -233,10 +235,13 @@
     visc,
     stress,
     pool_hbm,
+    owner_hbm,
+    mask_hbm,
     new_v,
     state,
     pooled,
     pool,
+    weights,
     coef,
     gsrc,
     ua,
@@ -244,10 +249,15 @@
     s_sum,
     flux,
     xmat,
+    owner,
+    mask,
     sem,
 ):
-    pool_copy = pltpu.make_async_copy(pool_hbm, pool, sem)
-    pool_copy.start()
+    pool_copy = pltpu.make_async_copy(pool_hbm, pool, sem.at[0])
+    owner_copy = pltpu.make_async_copy(owner_hbm, owner, sem.at[1])
+    mask_copy = pltpu.make_async_copy(mask_hbm, mask, sem.at[2])
+    for c in (pool_copy, owner_copy, mask_copy):
+        c.start()
     planes = visc.shape[0] // CY
     cz = visc.shape[1]
 
@@ -344,6 +354,18 @@
             cols = slice(j * cz, (j + 1) * cz)
             xmat[k * ROWS_C : k * ROWS_C + 4, cols] = jnp.zeros((4, cz), jnp.float32)
             xmat[k * ROWS_C + 8 : k * ROWS_C + HALF + 4, cols] = 0.125 * both[2 : HALF - 2]
+    owner_copy.wait()
+    mask_copy.wait()
+    me = lax.axis_index("wide")
+    for d in range(weights.shape[0] // (P_SIZE + 1)):
+        local = jnp.float32(-1.0)
+        for p in range(P_SIZE):
+            match = owner[0, p] // CP_DEV == me ^ d
+            weight = jnp.where(match, mask[0, p], 0).astype(jnp.float32)
+            local = jnp.where(match, (owner[0, p] % CP_DEV).astype(jnp.float32), local)
+            weights[d * (P_SIZE + 1) + p] = jnp.full((8, cz), weight, jnp.float32)
+        weights[d * (P_SIZE + 1) + P_SIZE] = jnp.full((8, cz), local, jnp.float32)
+
     pool_copy.wait()
     pooled[...] = split_dot(xmat[...], pool[...])
 
@@ -369,8 +391,7 @@
 
 def edge_kernel(
     n_wide,
-    owner,
-    mask,
+    weights,
     own,
     got_a,
     got_b,
@@ -380,38 +401,24 @@
     state,
     pooled,
     pool,
-    velocity_in,
-    velocity_out,
+    u_out,
     *refs,
 ):
     slots = refs[:n_wide]
-    u_out, xmat, flux, out_sem = refs[n_wide:]
-    rows = velocity_out.shape[1]
-    inner = pl.ds(SWEEPS * CY, rows - 2 * SWEEPS * CY)
-    inner_copy = pltpu.make_async_copy(
-        velocity_in.at[:, inner], velocity_out.at[:, inner], out_sem.at[2]
-    )
-    inner_copy.start()
+    xmat, flux = refs[n_wide:]
+    rows = visc.shape[0]
     grp = lax.axis_index("grp")
     even = grp % 2 == 0
     ends = (grp > 0, grp < lax.axis_size("grp") - 1)
     cz = pool.shape[0] // 4
 
-    me = lax.axis_index("wide")
-    weights = []
     for d in range(n_wide):
-        local, weight = jnp.float32(-1.0), []
-        for p in range(P_SIZE):
-            match = owner[0, p] // CP_DEV == me ^ d
-            weight.append(jnp.where(match, mask[0, p], 0).astype(jnp.float32))
-            local = jnp.where(match, (owner[0, p] % CP_DEV).astype(jnp.float32), local)
-        weights.append(weight)
-        slots[d][3 * ROWS_C :, :] = jnp.full((8, cz), local, jnp.float32)
+        slots[d][3 * ROWS_C :, :] = weights[d * (P_SIZE + 1) + P_SIZE]
 
     def weighted(d, value):
         total = None
         for p in range(P_SIZE):
-            term = value[:, p * cz : (p + 1) * cz] * weights[d][p]
+            term = value[:, p * cz : (p + 1) * cz] * weights[d * (P_SIZE + 1) + p, 0:1, :]
             total = term if total is None else total + term
         return total
 
@@ -505,41 +512,52 @@
                         flux[side, k, face, 2 * j : 2 * j + 1, :]
                         + flux[side, k, face, 2 * j + 1 : 2 * j + 2, :]
                     )
-    out_copies = [
-        pltpu.make_async_copy(
-            u_out.at[side],
-            velocity_out.at[:, pl.ds(0 if side == 0 else rows - SWEEPS * CY, SWEEPS * CY)],
-            out_sem.at[side],
-        )
-        for side in range(2)
-    ]
-    for c in out_copies:
-        c.start()
-
     edge = split_dot(xmat[...], pool[...])
     for k in range(3):
         part = slice(k * ROWS_C, k * ROWS_C + 8)
         value = pooled[part, :] + edge[k * 8 : (k + 1) * 8]
         for d in range(n_wide):
             slots[d][part, :] = weighted(d, value)
-    for c in out_copies:
+
+
+def velocity_kernel(inner, edges, out, sem):
+    rows, rim = out.shape[1], edges.shape[2]
+    mid = pl.ds(rim, rows - 2 * rim)
+    copies = [
+        pltpu.make_async_copy(inner.at[:, mid], out.at[:, mid], sem.at[0]),
+        pltpu.make_async_copy(edges.at[0], out.at[:, pl.ds(0, rim)], sem.at[1]),
+        pltpu.make_async_copy(edges.at[1], out.at[:, pl.ds(rows - rim, rim)], sem.at[2]),
+    ]
+    for c in copies:
+        c.start()
+    for c in copies:
         c.wait()
-    inner_copy.wait()
 
 
 def collect_kernel(n_wide, *refs):
-    slots, out = refs[:n_wide], refs[n_wide]
+    slots, out, (block, sem) = refs[:n_wide], refs[n_wide], refs[n_wide + 1 :]
     cz = slots[0].shape[1]
     rows = lax.broadcasted_iota(jnp.int32, (CP_DEV, cz), 0).astype(jnp.float32)
     takes = [rows == slot[3 * ROWS_C : 3 * ROWS_C + 1, :] for slot in slots]
+    width = PV // PIECES
+    place_of = {n: place for place, n in enumerate(ROW_ORDER)}
+    copies = []
     for k in range(3):
-        for place, n in enumerate(ROW_ORDER):
-            total = None
-            for take, slot in zip(takes, slots, strict=True):
-                r = k * ROWS_C + place
-                term = jnp.where(take, slot[r : r + 1, :], 0.0)
-                total = term if total is None else total + term
-            out[k, :, n * cz : (n + 1) * cz] = total
+        for piece in range(PIECES):
+            for n in range(piece * width // cz, (piece + 1) * width // cz):
+                total = None
+                for take, slot in zip(takes, slots, strict=True):
+                    r = k * ROWS_C + place_of[n]
+                    term = jnp.where(take, slot[r : r + 1, :], 0.0)
+                    total = term if total is None else total + term
+                block[k, :, n * cz : (n + 1) * cz] = total
+            part = (k, slice(None), pl.ds(piece * width, width))
+            copies.append(
+                pltpu.make_async_copy(block.at[part], out.at[part], sem.at[k * PIECES + piece])
+            )
+            copies[-1].start()
+    for c in copies:
+        c.wait()
 
 
 def on_device(velocity, coarse_ghost, viscosity, stress, patch_mask, coarse_owner):
@@ -554,7 +572,6 @@
 
     anywhere = pl.BlockSpec(memory_space=pltpu.HBM)
     vmem = pl.BlockSpec(memory_space=pltpu.VMEM)
-    smem = pl.BlockSpec(memory_space=pltpu.SMEM)
     pack_shape = jax.ShapeDtypeStruct((PACK, cz), f32)
     pack_a, pack_b, own = pl.pallas_call(
         pack_kernel,
@@ -578,16 +595,17 @@
     got_a = lax.ppermute(pack_a, "grp", pairs_a)
 
     rows = cells_x * CY
-    new_v, state, pooled, pool = pl.pallas_call(
+    new_v, state, pooled, pool, weights = pl.pallas_call(
         interior_kernel,
         out_shape=(
             jax.ShapeDtypeStruct((3, rows, cz), f32),
             jax.ShapeDtypeStruct((2, STATE * CY, cz), f32),
             jax.ShapeDtypeStruct((3 * ROWS_C, P_SIZE * cz), f32),
             jax.ShapeDtypeStruct(pool.shape, pool.dtype),
+            jax.ShapeDtypeStruct((n_wide * (P_SIZE + 1), 8, cz), f32),
         ),
-        in_specs=[vmem] * 4 + [anywhere],
-        out_specs=(vmem, vmem, vmem, vmem),
+        in_specs=[vmem] * 4 + [anywhere] * 3,
+        out_specs=(vmem,) * 5,
         scratch_shapes=[
             pltpu.VMEM((7, rows, cz), f32),
             pltpu.VMEM((3, rows, cz), f32),
@@ -596,29 +614,46 @@
             pltpu.VMEM((3, rows // 2, cz), f32),
             pltpu.VMEM((cells_x, cz), f32),
             pltpu.VMEM((3 * ROWS_C, 4 * cz), f32),
-            pltpu.SemaphoreType.DMA,
+            pltpu.SMEM((1, P_SIZE), jnp.int32),
+            pltpu.SMEM((1, P_SIZE), jnp.int32),
+            pltpu.SemaphoreType.DMA((3,)),
         ],
         cost_estimate=pl.CostEstimate(flops=100_000_000, bytes_accessed=4_000_000, transcendentals=0),
         compiler_params=pltpu.CompilerParams(vmem_limit_bytes=20 * 2**20),
         name="interior",
-    )(vel, ghost, visc, strs, pltpu.with_memory_space_constraint(pool, pltpu.HBM))
+    )(
+        vel,
+        ghost,
+        visc,
+        strs,
+        *(pltpu.with_memory_space_constraint(x, pltpu.HBM) for x in (pool, coarse_owner, patch_mask)),
+    )
 
     slot_shape = jax.ShapeDtypeStruct((SLOT, cz), f32)
+    rim_shape = jax.ShapeDtypeStruct((2, 3, SWEEPS * CY, cz), f32)
     outs = pl.pallas_call(
         functools.partial(edge_kernel, n_wide),
-        out_shape=(jax.ShapeDtypeStruct(new_v.shape, f32),) + (slot_shape,) * n_wide,
-        in_specs=[smem, smem] + [vmem] * 10,
-        out_specs=(anywhere,) + (vmem,) * n_wide,
+        out_shape=(rim_shape,) + (slot_shape,) * n_wide,
+        in_specs=[vmem] * 10,
+        out_specs=(vmem,) * (1 + n_wide),
         scratch_shapes=[
-            pltpu.VMEM((2, 3, 3 * CY, cz), f32),
             pltpu.VMEM((24, 4 * cz), f32),
             pltpu.VMEM((2, 3, 2, 8, cz), f32),
-            pltpu.SemaphoreType.DMA((3,)),
         ],
         compiler_params=pltpu.CompilerParams(vmem_limit_bytes=8 * 2**20),
         name="edge",
-    )(coarse_owner, patch_mask, own, got_a, got_b, vel, ghost, visc, state, pooled, pool, new_v)
-    smoothed, slots = outs[0], list(outs[1:])
+    )(weights, own, got_a, got_b, vel, ghost, visc, state, pooled, pool)
+    slots = list(outs[1:])
+    smoothed = pl.pallas_call(
+        velocity_kernel,
+        out_shape=jax.ShapeDtypeStruct(new_v.shape, f32),
+        in_specs=[vmem, vmem],
+        out_specs=anywhere,
+        scratch_shapes=[pltpu.SemaphoreType.DMA((3,))],
+        cost_estimate=pl.CostEstimate(flops=20_000_000, bytes_accessed=1_600_000, transcendentals=0),
+        compiler_params=pltpu.CompilerParams(vmem_limit_bytes=4 * 2**20),
+        name="velocity",
+    )(new_v, outs[0])
 
     for k in range(1, n_wide):
         slots[k] = lax.ppermute(slots[k], "wide", [(i, i ^ k) for i in range(n_wide)])
@@ -626,7 +661,11 @@
         functools.partial(collect_kernel, n_wide),
         out_shape=jax.ShapeDtypeStruct((3, CP_DEV, PV), f32),
         in_specs=[vmem] * n_wide,
-        out_specs=vmem,
+        out_specs=anywhere,
+        scratch_shapes=[
+            pltpu.VMEM((3, CP_DEV, PV), f32),
+            pltpu.SemaphoreType.DMA((3 * PIECES,)),
+        ],
         compiler_params=pltpu.CompilerParams(vmem_limit_bytes=8 * 2**20),
         name="collect",
     )(*slots)

time: 20.9 us -> 19.4 us (0.928)
  waiting for transfers between devices: 4.15 us -> 3.25 us
  Pallas kernels: 8.22 us -> 7.69 us
    ppermute x3, waiting for transfers between devices: 4.15 us -> 3.24 us  [on_device(): lax.ppermute(slots[k], 'wide', [(i, i ^ k) for i in range(n_wide)])]
    pallas_call x1 -> x2, Pallas kernels: 1.93 us -> 1.51 us  [the longest x1 0.89 us: on_device(): pl.pallas_call(velocity_kernel, out_shape=jax.ShapeDtypeStruct(new_v.shap...]
  transfers between devices with their start and end apart: 5 -> 5, of which waited for: 2 -> 2; matrix products, arithmetic and copies ran while one was open for 0% -> 0% of each run, Pallas kernels for 17% -> 23%
where the time goes in v3:
time: 19.4 us; the launch traced here: 19.2 us
  Pallas kernels  7.69 us (40%)
  starting transfers between devices  7.45 us (38%)
  waiting for transfers between devices  3.25 us (17%)
  between operations  0.76 us (4%)
    ppermute x1, starting transfers between devices, on_device(): got_b = lax.ppermute(pack_b, 'grp', pairs_b)  4.12 us
    pallas_call x1, Pallas kernels, on_device(): pl.pallas_call(interior_kernel, out_shape=(jax.ShapeDtypeStruct((3, rows,...  3.6 us
    ppermute x3, waiting for transfers between devices, on_device(): lax.ppermute(slots[k], 'wide', [(i, i ^ k) for i in range(n_wide)])  3.24 us
    ppermute x3, starting transfers between devices, on_device(): lax.ppermute(slots[k], 'wide', [(i, i ^ k) for i in range(n_wide)])  3.01 us
    pallas_call x1, Pallas kernels, on_device(): pl.pallas_call(pack_kernel, out_shape=(pack_shape, pack_shape, jax.ShapeD...  1.47 us
    pallas_call x1, Pallas kernels, on_device(): pl.pallas_call(functools.partial(collect_kernel, n_wide), out_shape=jax.S...  1.1 us
    pallas_call x1, Pallas kernels, on_device(): pl.pallas_call(velocity_kernel, out_shape=jax.ShapeDtypeStruct(new_v.shap...  0.89 us
    pallas_call x1, Pallas kernels, on_device(): pl.pallas_call(functools.partial(edge_kernel, n_wide), out_shape=(rim_sha...  0.62 us
  transfers between devices with their start and end apart: 5, of which 2 were waited for; matrix products, arithmetic and copies ran while one was open for 0% of the time, Pallas kernels for 23%

profile of v3, /device:TPU:11, one launch (start us, length us, event | category | flops | bytes accessed | tf_op | source)
XLA Modules:
  0.0 19.2 jit_solution(10707440306066688710)
XLA Ops:
  0.6 0.0 copy-start.1
  0.6 0.0 copy-start.2
  0.7 0.0 copy-start.3
  0.7 0.0 copy-start
  0.7 1.5 %pack.1 = (f32[152,128]{1,0:T(8,128)S(1)}, f32[152,128]{1,0:T(8,128)S(1)}, f32[2,48,128]{2,1,0:T(8,128)S(1)}) custom-call(f32[3,512,128]{2,1,0:T(8,128)} %bitcast.8, f32[3,128,128]{2,1,0:T(8,128)} %bitcast.16, f32[512,128]{1,0:T(8,128)} %bitcast.13, f32[6,512,128]{2,1,0:T(8,128)} %bitcast.11), custom_call_target="tpu_custom_call" | custom-call | tf_op jit(solution)/shard_map/pack/pallas_call | solution.py:576
  2.1 0.3 %collective-permute-start = (f32[152,128]{1,0:T(8,128)S(1)}, f32[152,128]{1,0:T(8,128)S(1)}, u32[]{:S(2)}, u32[]{:S(2)}) collective-permute-start(f32[152,128]{1,0:T(8,128)S(1)} %get-tuple-element.18), channel_id=1, source_target_pairs={{0,4},{4,0},{8,12},{12,8},{16,20},{20,16},{24,28},{28,24},{1,5},{5... | collective-permute-start | bytes 233480 | tf_op jit(solution)/shard_map/ppermute | solution.py:595
  2.5 4.1 %collective-permute-start.1 = (f32[152,128]{1,0:T(8,128)S(1)}, f32[152,128]{1,0:T(8,128)S(1)}, u32[]{:S(2)}, u32[]{:S(2)}) collective-permute-start(f32[152,128]{1,0:T(8,128)S(1)} %get-tuple-element.19), channel_id=1, source_target_pairs={{4,8},{8,4},{12,16},{16,12},{20,24},{24,20},{5,9},{9,5},{13,17},{1... | collective-permute-start | bytes 233480 | tf_op jit(solution)/shard_map/ppermute | solution.py:594
  6.6 0.0 copy-done.1
  6.6 0.0 copy-done.2
  6.6 0.0 copy-done.3
  6.6 0.0 copy-done
  6.6 3.6 %interior.1 = (f32[3,512,128]{2,1,0:T(8,128)S(1)}, f32[2,384,128]{2,1,0:T(8,128)S(1)}, f32[144,256]{1,0:T(8,128)S(1)}, bf16[512,256]{1,0:T(8,128)(2,1)S(1)}, f32[12,8,128]{2,1,0:T(8,128)S(1)}) custom-call(f32[3,512,128]{2,1,0:T(8,128)S(1)} %bitcast.9, f32[3,128,128]{2,1,0:T(8,128)S(1)} %bitcast.17, f32[512,128]{1,0:T(8,128)S(1)} %bitcast.14, ...), custom_call_target="tpu_custom_call" | custom-call | flops 100000000 | bytes 4000000 | tf_op jit(solution)/shard_map/interior/pallas_call | solution.py:598
  10.3 0.0 collective-permute-done.got_a
  10.3 0.0 collective-permute-done.1.got_b
  10.3 0.6 %edge.1 = (f32[2,3,24,128]{3,2,1,0:T(8,128)S(1)}, f32[152,128]{1,0:T(8,128)S(1)}, f32[152,128]{1,0:T(8,128)S(1)}, f32[152,128]{1,0:T(8,128)S(1)}, f32[152,128]{1,0:T(8,128)S(1)}) custom-call(f32[12,8,128]{2,1,0:T(8,128)S(1)} %get-tuple-element.16.weights, f32[2,48,128]{2,1,0:T(8,128)S(1)} %get-tuple-element.17.own, ...), custom_call_target="tpu_custom_call" | custom-call | tf_op jit(solution)/shard_map/edge/pallas_call | solution.py:634
  10.9 1.3 %collective-permute-start.2 = (f32[152,128]{1,0:T(8,128)S(1)}, f32[152,128]{1,0:T(8,128)S(1)}, u32[]{:S(2)}, u32[]{:S(2)}) collective-permute-start(f32[152,128]{1,0:T(8,128)S(1)} %get-tuple-element.25), channel_id=1, source_target_pairs={{0,1},{1,0},{2,3},{3,2},{4,5},{5,4},{6,7},{7,6},{8,9},{9,8},{10,11... | collective-permute-start | bytes 233480 | tf_op jit(solution)/shard_map/ppermute | solution.py:659
  12.2 1.2 %collective-permute-start.3 = (f32[152,128]{1,0:T(8,128)S(1)}, f32[152,128]{1,0:T(8,128)S(1)}, u32[]{:S(2)}, u32[]{:S(2)}) collective-permute-start(f32[152,128]{1,0:T(8,128)S(1)} %get-tuple-element.26), channel_id=1, source_target_pairs={{0,2},{1,3},{2,0},{3,1},{4,6},{5,7},{6,4},{7,5},{8,10},{9,11},{10,... | collective-permute-start | bytes 233480 | tf_op jit(solution)/shard_map/ppermute | solution.py:659
  13.4 0.5 %collective-permute-start.4 = (f32[152,128]{1,0:T(8,128)S(1)}, f32[152,128]{1,0:T(8,128)S(1)}, u32[]{:S(2)}, u32[]{:S(2)}) collective-permute-start(f32[152,128]{1,0:T(8,128)S(1)} %get-tuple-element.27), channel_id=1, source_target_pairs={{0,3},{1,2},{2,1},{3,0},{4,7},{5,6},{6,5},{7,4},{8,11},{9,10},{10,... | collective-permute-start | bytes 233480 | tf_op jit(solution)/shard_map/ppermute | solution.py:659
  13.9 0.9 %velocity.1 = f32[3,512,128]{2,1,0:T(8,128)} custom-call(f32[3,512,128]{2,1,0:T(8,128)S(1)} %get-tuple-element.15.inner, f32[2,3,24,128]{3,2,1,0:T(8,128)S(1)} %get-tuple-element.23.edges), custom_call_target="tpu_custom_call" | custom-call | flops 20000000 | bytes 1600000 | tf_op jit(solution)/shard_map/velocity/pallas_call | solution.py:647
  14.8 0.0 collective-permute-done.2.refs_1_
  14.8 1.2 %collective-permute-done.3.refs_2_ = f32[152,128]{1,0:T(8,128)S(1)} collective-permute-done((f32[152,128]{1,0:T(8,128)S(1)}, f32[152,128]{1,0:T(8,128)S(1)}, u32[]{:S(2)}, u32[]{:S(2)}) %collective-permute-start.3) | collective-permute-done | bytes 77856 | tf_op jit(solution)/shard_map/ppermute | solution.py:659
  16.0 2.0 %collective-permute-done.4.refs_3_ = f32[152,128]{1,0:T(8,128)S(1)} collective-permute-done((f32[152,128]{1,0:T(8,128)S(1)}, f32[152,128]{1,0:T(8,128)S(1)}, u32[]{:S(2)}, u32[]{:S(2)}) %collective-permute-start.4) | collective-permute-done | bytes 77856 | tf_op jit(solution)/shard_map/ppermute | solution.py:659
  18.1 1.1 %collect.1 = f32[3,16,6144]{2,1,0:T(8,128)} custom-call(f32[152,128]{1,0:T(8,128)S(1)} %get-tuple-element.24.refs_0_, f32[152,128]{1,0:T(8,128)S(1)} %collective-permute-done.2.refs_1_, f32[152,128]{1,0:T(8,128)S(1)} %collective-permute-done.3.refs_2_, f32[152,128]{1,0:T(8,128)S(1)} %collective-permute-done.4.refs_3_), custom_call_target="tpu_custom_call" | custom-call | tf_op jit(solution)/shard_map/collect/pallas_call | solution.py:660
Async XLA Ops:
  0.6 6.0 %copy-start.1 = (f32[6,64,8,128]{3,2,1,0:T(8,128)S(1)}, f32[6,64,8,128]{3,2,1,0:T(8,128)}, u32[]{:S(2)}) copy-start(f32[6,64,8,128]{3,2,1,0:T(8,128)} %param.10) | copy-start | bytes 4718596
  0.6 6.0 %copy-start.2 = (f32[64,8,128]{2,1,0:T(8,128)S(1)}, f32[64,8,128]{2,1,0:T(8,128)}, u32[]{:S(2)}) copy-start(f32[64,8,128]{2,1,0:T(8,128)} %param.9) | copy-start | bytes 786436
  0.7 6.0 %copy-start.3 = (f32[3,64,2,128]{3,2,1,0:T(2,128)S(1)}, f32[3,64,2,128]{3,2,1,0:T(2,128)}, u32[]{:S(2)}) copy-start(f32[3,64,2,128]{3,2,1,0:T(2,128)} %param.8) | copy-start | bytes 589828
  0.7 6.0 %copy-start = (f32[3,64,8,128]{3,2,1,0:T(8,128)S(1)}, f32[3,64,8,128]{3,2,1,0:T(8,128)}, u32[]{:S(2)}) copy-start(f32[3,64,8,128]{3,2,1,0:T(8,128)} %param.7) | copy-start | bytes 2359300
  2.1 8.1 %collective-permute-start = (f32[152,128]{1,0:T(8,128)S(1)}, f32[152,128]{1,0:T(8,128)S(1)}, u32[]{:S(2)}, u32[]{:S(2)}) collective-permute-start(f32[152,128]{1,0:T(8,128)S(1)} %get-tuple-element.18), channel_id=1, source_target_pairs={{0,4},{4,0},{8,12},{12,8},{16,20},{20,16},{24,28},{28,24},{1,5},{5... | collective-permute-start | bytes 233480 | tf_op jit(solution)/shard_map/ppermute | solution.py:595
  2.5 7.8 %collective-permute-start.1 = (f32[152,128]{1,0:T(8,128)S(1)}, f32[152,128]{1,0:T(8,128)S(1)}, u32[]{:S(2)}, u32[]{:S(2)}) collective-permute-start(f32[152,128]{1,0:T(8,128)S(1)} %get-tuple-element.19), channel_id=1, source_target_pairs={{4,8},{8,4},{12,16},{16,12},{20,24},{24,20},{5,9},{9,5},{13,17},{1... | collective-permute-start | bytes 233480 | tf_op jit(solution)/shard_map/ppermute | solution.py:594
  10.9 3.9 %collective-permute-start.2 = (f32[152,128]{1,0:T(8,128)S(1)}, f32[152,128]{1,0:T(8,128)S(1)}, u32[]{:S(2)}, u32[]{:S(2)}) collective-permute-start(f32[152,128]{1,0:T(8,128)S(1)} %get-tuple-element.25), channel_id=1, source_target_pairs={{0,1},{1,0},{2,3},{3,2},{4,5},{5,4},{6,7},{7,6},{8,9},{9,8},{10,11... | collective-permute-start | bytes 233480 | tf_op jit(solution)/shard_map/ppermute | solution.py:659
  12.2 3.8 %collective-permute-start.3 = (f32[152,128]{1,0:T(8,128)S(1)}, f32[152,128]{1,0:T(8,128)S(1)}, u32[]{:S(2)}, u32[]{:S(2)}) collective-permute-start(f32[152,128]{1,0:T(8,128)S(1)} %get-tuple-element.26), channel_id=1, source_target_pairs={{0,2},{1,3},{2,0},{3,1},{4,6},{5,7},{6,4},{7,5},{8,10},{9,11},{10,... | collective-permute-start | bytes 233480 | tf_op jit(solution)/shard_map/ppermute | solution.py:659
  13.4 4.6 %collective-permute-start.4 = (f32[152,128]{1,0:T(8,128)S(1)}, f32[152,128]{1,0:T(8,128)S(1)}, u32[]{:S(2)}, u32[]{:S(2)}) collective-permute-start(f32[152,128]{1,0:T(8,128)S(1)} %get-tuple-element.27), channel_id=1, source_target_pairs={{0,3},{1,2},{2,1},{3,0},{4,7},{5,6},{6,5},{7,4},{8,11},{9,10},{10,... | collective-permute-start | bytes 233480 | tf_op jit(solution)/shard_map/ppermute | solution.py:659
